TPU v7x, 32 devices: a 4x4x1 block of a 4x4x8 slice. The times are simulated.
32 devices in a mesh: rep: 1 (over z), tp: 4 (over y), sp: 8 (over x, core).
Axes of the slice: x: 4, y: 4, z: 1, core: 2. Of those that a mesh axis runs over, the one named last changes fastest.
The devices are a block of a 4x4x8 slice.
Arguments:
- x_tokens: bfloat16 [6144, 4096], P(('rep', 'sp'))
- positions: int32 [6144], P(('rep', 'sp'))
- gains: float32 [2, 4, 4096], replicated
- w_q: bfloat16 [2, 4096, 32, 128], P(None, None, 'tp')
- w_k: bfloat16 [2, 4096, 8, 128], P(None, None, 'tp')
- w_v: bfloat16 [2, 4096, 8, 128], P(None, None, 'tp')
- w_o: bfloat16 [2, 32, 128, 4096], P(None, 'tp')
- w_gate: bfloat16 [2, 4096, 14336], P(None, None, 'tp')
- w_up: bfloat16 [2, 4096, 14336], P(None, None, 'tp')
- w_down: bfloat16 [2, 14336, 4096], P(None, 'tp')
Outputs:
- output 1: bfloat16 [6144, 4096], P(('rep', 'sp'))
- output 2: bfloat16 [512, 32, 128], P('rep', ('tp', 'sp'))
- output 3: bfloat16 [512, 32, 128], P('rep', ('tp', 'sp'))
- output 4: bfloat16 [6144, 32, 128], P('rep', ('tp', 'sp'))
- output 5: bfloat16 [6144, 32, 128], P('rep', ('tp', 'sp'))
All inputs are finite; a program needn't handle non-finite values.
Results may differ from a plain program's by a relative error of at most 0.0162776.
Values are sent between devices in bfloat16 or wider.
A program may use at most 768 MiB of HBM per device.

v0:
```python
import jax
import jax.numpy as jnp
from jax import lax
from jax.sharding import PartitionSpec as P, NamedSharding

NORM_EPS = 1e-6
WINDOW = 512
Q_BLOCK = 256
LOCAL_BASE = 10000.0
GLOBAL_BASE = 1000000.0


def rms_norm(values, gain):
    wide = values.astype(jnp.float32)
    inv_rms = lax.rsqrt(jnp.mean(wide * wide, axis=-1, keepdims=True) + NORM_EPS)
    return wide * inv_rms * gain


def rotary(projected, positions, base):
    half = projected.shape[-1] // 2
    inv_freq = base ** (-jnp.arange(half, dtype=jnp.float32) / half)
    angles = positions.astype(jnp.float32)[..., None] * inv_freq
    cos_part = jnp.cos(angles)[..., None, :]
    sin_part = jnp.sin(angles)[..., None, :]
    first = projected[..., :half]
    second = projected[..., half:]
    return jnp.concatenate([first * cos_part - second * sin_part, second * cos_part + first * sin_part], axis=-1)


def attend(q_heads, k_heads, v_heads, q_first, local):
    total = k_heads.shape[0]
    span = WINDOW + Q_BLOCK if local else total
    scale = q_heads.shape[-1] ** -0.5

    def one_block(block_id):
        q_start = block_id * Q_BLOCK
        q_tile = lax.dynamic_slice_in_dim(q_heads, q_start, Q_BLOCK, 0)
        q_idx = q_first + q_start + jnp.arange(Q_BLOCK)
        k_start = jnp.clip(q_first + q_start - WINDOW, 0, total - span) if local else 0
        k_tile = lax.dynamic_slice_in_dim(k_heads, k_start, span, 0)
        v_tile = lax.dynamic_slice_in_dim(v_heads, k_start, span, 0)
        k_idx = k_start + jnp.arange(span)
        allowed = k_idx[None, :] <= q_idx[:, None]
        if local:
            allowed = allowed & (q_idx[:, None] - k_idx[None, :] < WINDOW)
        scores = jnp.einsum('qhgd,khd->hgqk', q_tile, k_tile, preferred_element_type=jnp.float32) * scale
        weights = jax.nn.softmax(jnp.where(allowed, scores, -1e30), axis=-1).astype(jnp.bfloat16)
        return jnp.einsum('hgqk,khd->qhgd', weights, v_tile, preferred_element_type=jnp.float32).astype(jnp.bfloat16)

    blocks = lax.map(one_block, jnp.arange(q_heads.shape[0] // Q_BLOCK))
    return blocks.reshape(q_heads.shape)


def solution(mesh):
    sp_size = mesh.shape['sp']

    def layer(x_loc, pos_loc, gain, w_q, w_k, w_v, w_o, w_gate, w_up, w_down, local):
        base = LOCAL_BASE if local else GLOBAL_BASE
        u_norm = rms_norm(x_loc, gain[0]).astype(jnp.bfloat16)
        q_rot = rotary(jnp.einsum('td,dhe->the', u_norm, w_q, preferred_element_type=jnp.float32), pos_loc, base).astype(jnp.bfloat16)
        k_rot = rotary(jnp.einsum('td,dhe->the', u_norm, w_k, preferred_element_type=jnp.float32), pos_loc, base).astype(jnp.bfloat16)
        v_new = jnp.einsum('td,dhe->the', u_norm, w_v, preferred_element_type=jnp.float32).astype(jnp.bfloat16)
        seq_dev, heads_tp, head_dim = q_rot.shape
        kv_tp = k_rot.shape[1]
        heads_dev = heads_tp // sp_size
        cache_dev = max(kv_tp // sp_size, 1)
        repeat = sp_size * cache_dev // kv_tp
        outgoing = jnp.concatenate([
            q_rot.reshape(seq_dev, sp_size, heads_dev, head_dim),
            jnp.repeat(k_rot, repeat, axis=1).reshape(seq_dev, sp_size, cache_dev, head_dim),
            jnp.repeat(v_new, repeat, axis=1).reshape(seq_dev, sp_size, cache_dev, head_dim)], axis=2)
        received = lax.all_to_all(outgoing, 'sp', 1, 0, tiled=True)
        total = received.shape[0]
        received = received.reshape(total, heads_dev + 2 * cache_dev, head_dim)
        q_all = received[:, :heads_dev].reshape(total, cache_dev, heads_dev // cache_dev, head_dim)
        k_all = received[:, heads_dev:heads_dev + cache_dev]
        v_all = received[:, heads_dev + cache_dev:]
        attn_out = attend(q_all, k_all, v_all, 0, local).reshape(sp_size, seq_dev, heads_dev, head_dim)
        attn_back = lax.all_to_all(attn_out, 'sp', 0, 2, tiled=True).reshape(seq_dev, heads_tp, head_dim)
        o_sum = lax.psum(jnp.einsum('the,hed->td', attn_back, w_o, preferred_element_type=jnp.float32), 'tp')
        x_mid = (x_loc.astype(jnp.float32) + rms_norm(o_sum, gain[1])).astype(jnp.bfloat16)
        u_mlp = rms_norm(x_mid, gain[2]).astype(jnp.bfloat16)
        gate_pre = jnp.dot(u_mlp, w_gate, preferred_element_type=jnp.float32)
        up_pre = jnp.dot(u_mlp, w_up, preferred_element_type=jnp.float32)
        hidden_act = (jax.nn.silu(gate_pre) * up_pre).astype(jnp.bfloat16)
        m_sum = lax.psum(jnp.dot(hidden_act, w_down, preferred_element_type=jnp.float32), 'tp')
        x_out = (x_mid.astype(jnp.float32) + rms_norm(m_sum, gain[3])).astype(jnp.bfloat16)
        if local:
            return x_out, k_all[total - WINDOW:], v_all[total - WINDOW:]
        return x_out, k_all, v_all

    def device_fn(x_loc, pos_loc, gains, w_q, w_k, w_v, w_o, w_gate, w_up, w_down):
        hidden, k_local, v_local = layer(x_loc, pos_loc, gains[0], w_q[0], w_k[0], w_v[0], w_o[0], w_gate[0], w_up[0], w_down[0], True)
        out_hidden, k_global, v_global = layer(hidden, pos_loc, gains[1], w_q[1], w_k[1], w_v[1], w_o[1], w_gate[1], w_up[1], w_down[1], False)
        return out_hidden, k_local, v_local, k_global, v_global

    token_spec = P(('rep', 'sp'), None)
    cache_spec = P('rep', ('tp', 'sp'), None)
    in_specs = (token_spec, P(('rep', 'sp')), P(), P(None, None, 'tp', None), P(None, None, 'tp', None),
                P(None, None, 'tp', None), P(None, 'tp', None, None), P(None, None, 'tp'), P(None, None, 'tp'),
                P(None, 'tp', None))
    out_specs = (token_spec, cache_spec, cache_spec, cache_spec, cache_spec)
    return jax.shard_map(device_fn, mesh=mesh, in_specs=in_specs, out_specs=out_specs, check_vma=False)
```

profile of v0, /device:TPU:97, one launch (start us, length us, event | category | flops | bytes accessed | tf_op | source)
XLA Modules:
  0.0 1707.3 jit_solution(14870090147635821070)
XLA Ops:
  8.1 4.5 fusion.57
  13.3 4.1 fusion.129
  17.4 6.4 copy.60
  23.8 6.3 fusion.130
  34.2 11.3 fusion.126
  45.5 11.9 copy.59
  57.4 11.2 fusion.119
  68.6 2.2 multiply_cosine_fusion
  72.1 2.6 copy.47
  74.7 6.5 all-to-all-start
  81.2 54.3 %all-to-all-done = bf16[768,8,3,128]{0,3,2,1:T(8,128)(2,1)} async-done(((bf16[768,8,3,128]{0,3,2,1:T(8,128)(2,1)}), bf16[768,8,3,128]{0,3,2,1:T(8,128)(2,1)}, u32[]{:S(2)}, u32[]{:S(2)}) %all-to-all-start) | async-done | bytes 4718624 | tf_op jit(solution)/shard_map/all_to_all | solution.py:72
  135.5 6.8 copy.48
  142.3 3.8 slice_bitcast_fusion.1
  146.1 91.8 %while.22 = (s32[]{:T(128)}, bf16[24,256,1,1,128]{4,1,0,3,2:T(8,128)(2,1)}, s32[24]{0:T(128)S(1)}, bf16[6144,1,128]{2,0,1:T(8,128)(2,1)}, bf16[6144,1,128]{2,0,1...) while((s32[]{:T(128)}, ...), condition=%wide.region_4.5_spmd, body=%wide.region_1.4_spmd.sunk | while | flops 103055880 | bytes 3160307 | solution.py:50
  237.9 25.0 %all_to_all.60 = bf16[8,768,1,128]{3,1,2,0:T(8,128)(2,1)S(1)} all-to-all(bf16[8,768,1,128]{3,1,2,0:T(8,128)(2,1)} %bitcast.244), channel_id=1, replica_groups=mesh['rep'=1,'tp'=4,'sp'=8] {'sp'}, dimensions={0} | all-to-all | bytes 3145728 | tf_op jit(solution)/shard_map/all_to_all | solution.py:79
  262.9 11.6 fusion.83
  274.6 223.4 %all-reduce.5.cloned.1.call-done = f32[768,4096]{1,0:T(8,128)} async-done(((f32[768,4096]{1,0:T(8,128)}), f32[768,4096]{1,0:T(8,128)}) %all-reduce.5.cloned.1.call-update) | async-done | bytes 12582928 | tf_op jit(solution)/shard_map/psum | solution.py:80
  498.0 5.6 multiply_reduce_fusion.3
  503.6 2.5 copy-done.3
  506.1 5.8 fusion.61
  512.0 2.7 copy-done.5
  514.7 27.7 %fusion.49 = f32[768,3584]{1,0:T(8,128)} fusion(bf16[2,4096,3584]{2,1,0:T(8,128)(2,1)} %param.21, bf16[768,4096]{1,0:T(8,128)(2,1)S(1)} %get-tuple-element.169, f32[4096]{0:T(1024)S(1)} %bitcast.256, f32[768]{0:T(1024)S(1)} %add_rsqrt_fusion.5), kind=kOutput, calls=%fused_computation.50 | convolution fusion | flops 22561161216 | bytes 46681088 | tf_op jit(solution)/shard_map/dot_general | solution.py:83
  542.3 34.2 %multiply_convert_fusion.1 = bf16[768,3584]{1,0:T(8,128)(2,1)} fusion(f32[768,3584]{1,0:T(8,128)} %fusion.49, bf16[2,4096,3584]{2,1,0:T(8,128)(2,1)} %param.22, bf16[768,4096]{1,0:T(8,128)(2,1)} %copy-done.5, f32[4096]{0:T(1024)S(1)} %bitcast.257, f32[768]{0:T(1024)S(1)} %add_rsqrt_fusion.5), kind=kOutput, calls=%fused_computation.91 | convolution fusion | flops 22577676288 | bytes 52186112 | tf_op jit(solution)/shard_map/dot_general | solution.py:84
  576.5 30.1 %fusion.45 = f32[768,4096]{1,0:T(8,128)} fusion(bf16[768,3584]{1,0:T(8,128)(2,1)} %multiply_convert_fusion.1, bf16[2,3584,4096]{2,1,0:T(8,128)(2,1)} %param.23), kind=kOutput, calls=%fused_computation.46 | convolution fusion | flops 22548578304 | bytes 47448064 | tf_op jit(solution)/shard_map/dot_general | solution.py:86
  608.2 4.0 copy.63
  612.1 11.9 copy.62
  624.0 205.4 %all-reduce.7.cloned.1.call-done = f32[768,4096]{1,0:T(8,128)} async-done(((f32[768,4096]{1,0:T(8,128)}), f32[768,4096]{1,0:T(8,128)}) %all-reduce.7.cloned.1.call-update) | async-done | bytes 12582928 | tf_op jit(solution)/shard_map/psum | solution.py:86
  829.4 5.6 multiply_reduce_fusion.2
  835.0 2.5 copy-done
  837.5 5.8 fusion.65
  843.4 11.9 fusion.114
  855.3 2.7 fusion.102
  858.0 2.9 fusion.112
  865.3 2.6 copy.55
  867.9 5.4 all-to-all-start.2
  873.3 54.3 %all-to-all-done.2 = bf16[768,8,3,128]{0,3,2,1:T(8,128)(2,1)} async-done(((bf16[768,8,3,128]{0,3,2,1:T(8,128)(2,1)}), bf16[768,8,3,128]{0,3,2,1:T(8,128)(2,1)}, u32[]{:S(2)}, u32[]{:S(2)}) %all-to-all-start.2) | async-done | bytes 4718624 | tf_op jit(solution)/shard_map/all_to_all | solution.py:72
  927.6 6.7 copy.56
  934.3 3.8 fusion.128
  938.1 157.6 %while.23 = (s32[]{:T(128)}, bf16[24,256,1,1,128]{4,1,3,2,0:T(8,128)(2,1)}, s32[24]{0:T(128)S(1)}, bf16[6144,1,1,128]{3,0,2,1:T(8,128)(2,1)}, bf16[6144,1,128]{2...) while((s32[]{:T(128)}, ...), condition=%wide.region_14.15_spmd, body=%wide.region_11.14_spmd.sunk | while | flops 819494656 | bytes 22158516 | solution.py:50
  939.4 2.2 fusion.155
  965.6 2.2 fusion.155
  972.2 2.2 fusion.155
  1005.0 2.2 fusion.155
  1024.7 2.2 fusion.155
  1031.3 2.2 fusion.155
  1044.5 2.2 fusion.155
  1051.0 2.2 fusion.155
  1057.6 2.2 fusion.155
  1064.2 2.2 fusion.155
  1070.7 2.2 fusion.155
  1095.8 25.0 %all_to_all.61 = bf16[8,768,1,128]{3,1,2,0:T(8,128)(2,1)S(1)} all-to-all(bf16[8,768,1,128]{3,1,2,0:T(8,128)(2,1)} %bitcast.243), channel_id=1, replica_groups=mesh['rep'=1,'tp'=4,'sp'=8] {'sp'}, dimensions={0} | all-to-all | bytes 3145728 | tf_op jit(solution)/shard_map/all_to_all | solution.py:79
  1120.7 11.6 fusion.86
  1132.7 220.8 %all-reduce.9.cloned.1.call-done = f32[768,4096]{1,0:T(8,128)} async-done(((f32[768,4096]{1,0:T(8,128)}), f32[768,4096]{1,0:T(8,128)}) %all-reduce.9.cloned.1.call-update) | async-done | bytes 12582928 | tf_op jit(solution)/shard_map/psum | solution.py:80
  1353.5 5.6 multiply_reduce_fusion.1
  1359.1 2.5 copy-done.2
  1361.6 5.8 fusion.69
  1367.5 2.7 copy-done.6
  1370.2 27.6 %fusion.43 = f32[768,3584]{1,0:T(8,128)} fusion(bf16[2,4096,3584]{2,1,0:T(8,128)(2,1)} %param.21, bf16[768,4096]{1,0:T(8,128)(2,1)S(1)} %get-tuple-element.165, f32[4096]{0:T(1024)S(1)} %bitcast.251, f32[768]{0:T(1024)S(1)} %add_rsqrt_fusion.1), kind=kOutput, calls=%fused_computation.44 | convolution fusion | flops 22561161216 | bytes 46681088 | tf_op jit(solution)/shard_map/dot_general | solution.py:83
  1397.8 33.8 %multiply_convert_fusion = bf16[768,3584]{1,0:T(8,128)(2,1)} fusion(f32[768,3584]{1,0:T(8,128)} %fusion.43, bf16[2,4096,3584]{2,1,0:T(8,128)(2,1)} %param.22, bf16[768,4096]{1,0:T(8,128)(2,1)} %copy-done.6, f32[4096]{0:T(1024)S(1)} %bitcast.252, f32[768]{0:T(1024)S(1)} %add_rsqrt_fusion.1), kind=kOutput, calls=%fused_computation.90 | convolution fusion | flops 22577676288 | bytes 52186112 | tf_op jit(solution)/shard_map/dot_general | solution.py:84
  1431.6 29.9 %fusion.39 = f32[768,4096]{1,0:T(8,128)} fusion(bf16[768,3584]{1,0:T(8,128)(2,1)} %multiply_convert_fusion, bf16[2,3584,4096]{2,1,0:T(8,128)(2,1)} %param.23), kind=kOutput, calls=%fused_computation.40 | convolution fusion | flops 22548578304 | bytes 47448064 | tf_op jit(solution)/shard_map/dot_general | solution.py:86
  1463.3 221.0 %all-reduce.11.cloned.1.call-done = f32[768,4096]{1,0:T(8,128)} async-done(((f32[768,4096]{1,0:T(8,128)}), f32[768,4096]{1,0:T(8,128)}) %all-reduce.11.cloned.1.call-update) | async-done | bytes 12582928 | tf_op jit(solution)/shard_map/psum | solution.py:86
  1684.3 5.6 multiply_reduce_fusion
  1690.0 2.5 copy-done.1
  1692.5 7.9 fusion.72
  (386 shorter events, 207.9 us)
Async XLA Ops:
  7.2 5.4 copy-start.17
  7.2 6.1 copy-start.8
  17.4 12.7 slice-start
  23.8 6.3 slice-start.1
  23.8 6.3 copy-start.10
  74.7 60.8 %all-to-all-start = ((bf16[768,8,3,128]{0,3,2,1:T(8,128)(2,1)}), bf16[768,8,3,128]{0,3,2,1:T(8,128)(2,1)}, u32[]{:S(2)}, u32[]{:S(2)}) async-start(bf16[768,8,3,128]{0,3,2,1:T(8,128)(2,1)} %copy.47), calls=%async_computation | async-start | bytes 9437184 | tf_op jit(solution)/shard_map/all_to_all | solution.py:72
  81.2 416.8 %all-reduce.5.cloned.1.call-start = ((), (), s32[]{:S(2)}) async-start(), calls=%async_computation.4 | async-start | bytes 25165824 | tf_op jit(solution)/shard_map/psum | solution.py:80
  274.5 554.9 %all-reduce.7.cloned.1.call-start = ((), (), s32[]{:S(2)}) async-start(), calls=%async_computation.5 | async-start | bytes 25165824 | tf_op jit(solution)/shard_map/psum | solution.py:86
  498.0 8.2 copy-start.3
  512.0 2.7 copy-start.5
  606.6 1.6 copy-start.7
  612.1 222.9 %copy-start.20 = (f32[1,1,4096]{2,1,0:T(1,128)S(1)}, f32[1,1,4096]{2,1,0:T(1,128)}, u32[]{:S(2)}) copy-start(f32[1,1,4096]{2,1,0:T(1,128)} %get-tuple-element.199) | copy-start | bytes 49156
  829.4 8.2 copy-start
  837.5 5.9 copy-start.22
  843.4 14.6 copy-start.4
  843.4 11.9 copy-start.11
  855.3 2.7 copy-start.9
  858.0 4.9 copy-start.12
  858.0 4.9 copy-start.13
  862.9 1.7 copy-start.16
  867.9 59.7 %all-to-all-start.2 = ((bf16[768,8,3,128]{0,3,2,1:T(8,128)(2,1)}), bf16[768,8,3,128]{0,3,2,1:T(8,128)(2,1)}, u32[]{:S(2)}, u32[]{:S(2)}) async-start(bf16[768,8,3,128]{0,3,2,1:T(8,128)(2,1)} %copy.55), calls=%async_computation.2 | async-start | bytes 9437184 | tf_op jit(solution)/shard_map/all_to_all | solution.py:72
  873.3 480.1 %all-reduce.9.cloned.1.call-start = ((), (), s32[]{:S(2)}) async-start(), calls=%async_computation.6 | async-start | bytes 25165824 | tf_op jit(solution)/shard_map/psum | solution.py:80
  1095.8 36.5 %copy-start.14 = (bf16[6144,1,128]{2,0,1:T(8,128)(2,1)}, bf16[6144,1,128]{2,0,1:T(8,128)(2,1)S(1)}, u32[]{:S(2)}) copy-start(bf16[6144,1,128]{2,0,1:T(8,128)(2,1)S(1)} %get-tuple-element.380) | copy-start | bytes 4718596
  1095.8 36.5 %copy-start.15 = (bf16[6144,1,128]{2,0,1:T(8,128)(2,1)}, bf16[6144,1,128]{2,0,1:T(8,128)(2,1)S(1)}, u32[]{:S(2)}) copy-start(bf16[6144,1,128]{2,0,1:T(8,128)(2,1)S(1)} %get-tuple-element.381) | copy-start | bytes 4718596
  1132.3 226.8 %copy-start.19 = (f32[1,1,4096]{2,1,0:T(1,128)S(1)}, f32[1,1,4096]{2,1,0:T(1,128)}, u32[]{:S(2)}) copy-start(f32[1,1,4096]{2,1,0:T(1,128)} %get-tuple-element.197) | copy-start | bytes 49156
  1132.4 552.0 %all-reduce.11.cloned.1.call-start = ((), (), s32[]{:S(2)}) async-start(), calls=%async_computation.7 | async-start | bytes 25165824 | tf_op jit(solution)/shard_map/psum | solution.py:86
  1353.5 8.2 copy-start.2
  1361.6 8.6 copy-start.21
  1367.5 2.7 copy-start.6
  1461.6 228.4 %copy-start.18 = (f32[1,1,4096]{2,1,0:T(1,128)S(1)}, f32[1,1,4096]{2,1,0:T(1,128)}, u32[]{:S(2)}) copy-start(f32[1,1,4096]{2,1,0:T(1,128)} %get-tuple-element.196) | copy-start | bytes 49156
  1684.3 8.2 copy-start.1
Sparse Core Ops, SparseCore 0:
  274.6 223.3 all-reduce.4
  606.7 222.5 all-reduce.6
  1132.5 220.9 all-reduce.8
  1461.7 222.5 all-reduce.10
where the time goes:
time: 1720 us; the launch traced here: 1710 us
  waiting for transfers between devices  979 us (57%)
  matrix products  381 us (22%)
  local copies, waits for them, and re-layouts  150 us (9%)
  other arithmetic  87.6 us (5%)
  blocking collectives  50 us (3%)
  loops' own time  32.6 us (2%)
    psum x2, waiting for transfers between devices, layer(): lax.psum(jnp.einsum('the,hed->td', attn_back, w_o, preferred_element_type...  444 us
    psum x2, waiting for transfers between devices, layer(): lax.psum(jnp.dot(hidden_act, w_down, preferred_element_type=jnp.float32),...  426 us
    all_to_all x2, waiting for transfers between devices, layer(): received = lax.all_to_all(outgoing, 'sp', 1, 0, tiled=True)  109 us
    dot_general x48, matrix products, one_block(): jnp.einsum('hgqk,khd->qhgd', weights, v_tile, preferred_element_type=jnp....  81 us
    dot_general x2, matrix products, layer(): up_pre = jnp.dot(u_mlp, w_up, preferred_element_type=jnp.float32)  68 us
    dot_general x48, matrix products, one_block(): jnp.einsum('qhgd,khd->hgqk', q_tile, k_tile, preferred_element_type=jnp.f...  60.9 us
    dot_general x2, matrix products, layer(): jnp.dot(hidden_act, w_down, preferred_element_type=jnp.float32)  60 us
    dot_general x2, matrix products, layer(): gate_pre = jnp.dot(u_mlp, w_gate, preferred_element_type=jnp.float32)  55.3 us
  transfers between devices with their start and end apart: 6, of which 6 were waited for; matrix products, arithmetic and copies ran while one was open for 1% of the time, Pallas kernels for 0%

commit v1 on v0

v1 whole, which is shorter than its diff:
```python
import functools
import math

import jax
import jax.numpy as jnp
from jax import lax
from jax.experimental import pallas as pl
from jax.experimental.pallas import tpu as pltpu
from jax.sharding import PartitionSpec as P

NORM_EPS = 1e-6
WINDOW = 512
Q_BLOCK = 256
LOCAL_BASE = 10000.0
GLOBAL_BASE = 1000000.0
CHUNKS = 2
PACK_ROWS = 512
NEG = -1e30
F32 = jnp.float32
BF16 = jnp.bfloat16


def rms_norm(values, gain):
    wide = values.astype(F32)
    inv_rms = lax.rsqrt(jnp.mean(wide * wide, axis=-1, keepdims=True) + NORM_EPS)
    return wide * inv_rms * gain


def rope_tables(positions, half, base):
    inv_freq = base ** (-jnp.arange(half, dtype=F32) / half)
    angles = positions.astype(F32)[:, None] * inv_freq
    cos_part, sin_part = jnp.cos(angles), jnp.sin(angles)
    return jnp.stack([jnp.concatenate([cos_part, cos_part], axis=1), jnp.concatenate([-sin_part, sin_part], axis=1)])


def pack_kernel(q_ref, k_ref, v_ref, out_ref):
    at = 0
    for ref in (q_ref, k_ref, v_ref):
        depth, heads, dim = ref.shape[1:]
        out_ref[:, at:at + heads * dim] = ref[0].reshape(depth, heads * dim)
        at += heads * dim


def pack_weights(w_q, w_k, w_v, layer):
    width, _, dim = w_q.shape[1:]
    heads = [w.shape[2] for w in (w_q, w_k, w_v)]
    depth = PACK_ROWS
    columns = sum(heads) * dim
    return pl.pallas_call(
        pack_kernel,
        grid=(width // depth,),
        in_specs=[pl.BlockSpec((1, depth, h, dim), lambda i: (layer, i, 0, 0)) for h in heads],
        out_specs=pl.BlockSpec((depth, columns), lambda i: (i, 0)),
        out_shape=jax.ShapeDtypeStruct((width, columns), BF16),
        compiler_params=pltpu.CompilerParams(vmem_limit_bytes=40 << 20),
        cost_estimate=pl.CostEstimate(flops=8 * width * columns, bytes_accessed=4 * width * columns, transcendentals=0),
        name='pack_weights',
    )(w_q, w_k, w_v)


def project_kernel(rotated, dim, u_ref, w_ref, table_ref, out_ref):
    product = jnp.dot(u_ref[...], w_ref[...], preferred_element_type=F32)
    heads = w_ref.shape[1] // dim

    @pl.when(pl.program_id(0) < rotated)
    def _():
        cos_part, sin_part = table_ref[0], table_ref[1]
        for h in range(heads):
            part = product[:, h * dim:(h + 1) * dim]
            out_ref[h] = (part * cos_part + pltpu.roll(part, dim // 2, 1) * sin_part).astype(BF16)

    @pl.when(pl.program_id(0) >= rotated)
    def _():
        for h in range(heads):
            out_ref[h] = product[:, h * dim:(h + 1) * dim].astype(BF16)


def project(u_norm, packed, tables, rotated_heads):
    rows, width = u_norm.shape
    dim = tables.shape[2]
    columns = packed.shape[1]
    step = 2
    return pl.pallas_call(
        functools.partial(project_kernel, rotated_heads // step, dim),
        grid=(columns // (step * dim),),
        in_specs=[pl.BlockSpec((rows, width), lambda i: (0, 0)), pl.BlockSpec((width, step * dim), lambda i: (0, i)),
                  pl.BlockSpec(tables.shape, lambda i: (0, 0, 0))],
        out_specs=pl.BlockSpec((step, rows, dim), lambda i: (i, 0, 0)),
        out_shape=jax.ShapeDtypeStruct((columns // dim, rows, dim), BF16),
        compiler_params=pltpu.CompilerParams(vmem_limit_bytes=40 << 20),
        cost_estimate=pl.CostEstimate(flops=2 * rows * width * columns, bytes_accessed=2 * width * (columns + rows), transcendentals=0),
        name='project',
    )(u_norm, packed, tables)


def local_kernel(scale2, first_ref, q_ref, k_ref, v_ref, out_ref):
    heads, rows, dim = q_ref.shape
    span = rows + WINDOW
    start = pl.multiple_of(pl.program_id(1) * rows, rows)
    k_tile = k_ref[0, pl.ds(start, span), :]
    v_tile = v_ref[0, pl.ds(start, span), :]
    q_idx = lax.broadcasted_iota(jnp.int32, (rows, span), 0)
    k_idx = lax.broadcasted_iota(jnp.int32, (rows, span), 1)
    allowed = (k_idx > q_idx) & (k_idx <= q_idx + WINDOW) & (k_idx + start >= first_ref[0])
    for head in range(heads):
        scores = lax.dot_general(q_ref[head], k_tile, (((1,), (1,)), ((), ())), preferred_element_type=F32) * scale2
        scores = jnp.where(allowed, scores, NEG)
        top = jnp.max(scores, axis=1, keepdims=True)
        weights = jnp.exp2(scores - top)
        weights = weights * (1.0 / jnp.sum(weights, axis=1, keepdims=True))
        out = jnp.dot(weights.astype(BF16), v_tile, preferred_element_type=F32)
        out_ref[:, head * dim:(head + 1) * dim] = out.astype(BF16)


def local_attention(first, qkv, kv_ext, kv_heads):
    tokens, dim = qkv.shape[1:]
    q_heads = qkv.shape[0] - 2 * kv_heads
    group = q_heads // kv_heads
    scale2 = dim ** -0.5 * math.log2(math.e)
    k_spec = pl.BlockSpec((1, WINDOW + tokens, dim), lambda h, i: (h, 0, 0))
    v_spec = pl.BlockSpec((1, WINDOW + tokens, dim), lambda h, i: (kv_heads + h, 0, 0))
    return pl.pallas_call(
        functools.partial(local_kernel, scale2),
        grid=(kv_heads, tokens // Q_BLOCK),
        in_specs=[pl.BlockSpec(memory_space=pltpu.SMEM), pl.BlockSpec((group, Q_BLOCK, dim), lambda h, i: (h, i, 0)),
                  k_spec, v_spec],
        out_specs=pl.BlockSpec((Q_BLOCK, group * dim), lambda h, i: (i, h)),
        out_shape=jax.ShapeDtypeStruct((tokens, q_heads * dim), BF16),
        compiler_params=pltpu.CompilerParams(vmem_limit_bytes=40 << 20),
        cost_estimate=pl.CostEstimate(flops=4 * tokens * q_heads * dim * (WINDOW + Q_BLOCK), bytes_accessed=8 * tokens * q_heads * dim,
                                      transcendentals=0),
        name='local_attention',
    )(first, qkv, kv_ext, kv_ext)


def global_kernel(scale2, chunk, k_block, q_ref, k_ref, v_ref, out_ref):
    rows, dim = q_ref.shape[2:]
    q_tile = q_ref[0, 0]

    def step(carry, k_tile, v_tile, mask):
        top, total, acc = carry
        scores = lax.dot_general(q_tile, k_tile, (((1,), (1,)), ((), ())), preferred_element_type=F32) * scale2
        if mask is not None:
            scores = jnp.where(mask, scores, NEG)
        new_top = jnp.maximum(top, jnp.max(scores, axis=1, keepdims=True))
        weights = jnp.exp2(scores - new_top)
        fix = jnp.exp2(top - new_top)
        total = total * fix + jnp.sum(weights, axis=1, keepdims=True)
        acc = acc * fix + jnp.dot(weights.astype(BF16), v_tile, preferred_element_type=F32)
        return new_top, total, acc

    shard = pl.program_id(0)
    base = pl.multiple_of(shard * k_block, k_block)
    width = (chunk + 1) * rows
    q_idx = lax.broadcasted_iota(jnp.int32, (rows, width), 0) + chunk * rows
    k_idx = lax.broadcasted_iota(jnp.int32, (rows, width), 1)
    carry = (jnp.full((rows, 1), NEG, F32), jnp.zeros((rows, 1), F32), jnp.zeros((rows, dim), F32))
    carry = step(carry, k_ref[pl.ds(base, width), :], v_ref[pl.ds(base, width), :], k_idx <= q_idx)

    def full(j, carry):
        at = pl.multiple_of(j * k_block, k_block)
        return step(carry, k_ref[pl.ds(at, k_block), :], v_ref[pl.ds(at, k_block), :], None)

    top, total, acc = lax.fori_loop(0, shard, full, carry)
    out_ref[0] = (acc / total).astype(BF16)


def global_attention(q_part, k_all, v_all, chunk):
    shards, _, rows, dim = q_part.shape
    total = k_all.shape[0]
    scale2 = dim ** -0.5 * math.log2(math.e)
    q_spec = pl.BlockSpec((1, 1, rows, dim), lambda s: (s, 0, 0, 0))
    out_spec = pl.BlockSpec((1, rows, dim), lambda s: (s, 0, 0))
    k_spec = pl.BlockSpec((total, dim), lambda s: (0, 0))
    return pl.pallas_call(
        functools.partial(global_kernel, scale2, chunk, total // shards),
        grid=(shards,),
        in_specs=[q_spec, k_spec, k_spec],
        out_specs=out_spec,
        out_shape=jax.ShapeDtypeStruct((shards, rows, dim), BF16),
        compiler_params=pltpu.CompilerParams(vmem_limit_bytes=40 << 20),
        cost_estimate=pl.CostEstimate(flops=4 * shards * rows * total * dim, bytes_accessed=8 * total * dim, transcendentals=0),
        name='global_attention',
    )(q_part, k_all, v_all)


def solution(mesh):
    sp_size = mesh.shape['sp']
    tp_size = mesh.shape['tp']

    barrier = lax.optimization_barrier

    def gather(rows):
        return lax.all_gather(rows, 'tp', axis=0, tiled=True)

    def finish(partial, residual, gain):
        summed = lax.psum_scatter(partial, 'tp', scatter_dimension=0, tiled=True)
        return (residual.astype(F32) + rms_norm(summed, gain)).astype(BF16)

    def mlp(u_mlp, w_gate, w_up, w_down):
        gate_pre = jnp.dot(u_mlp, w_gate, preferred_element_type=F32)
        up_pre = jnp.dot(u_mlp, w_up, preferred_element_type=F32)
        hidden_act = (jax.nn.silu(gate_pre) * up_pre).astype(BF16)
        return jnp.dot(hidden_act, w_down, preferred_element_type=F32)

    def after_attention(partial_of, residuals, gain, w_gate, w_up, w_down, send_of):
        mids, gathered, partials, sent = [], [], [], []
        for c in range(CHUNKS):
            o_partial = partial_of(c)
            if c > 0:
                gathered[-1], o_partial = barrier((gathered[-1], o_partial))
                partials.append(mlp(gathered[-1], w_gate, w_up, w_down))
            x_mid = finish(o_partial, residuals[c], gain[1])
            mids.append(x_mid)
            gathered.append(gather(rms_norm(x_mid, gain[2]).astype(BF16)))
        for c in range(CHUNKS):
            if c + 1 < CHUNKS:
                follow = gathered[-1]
                follow, partials[c] = barrier((follow, partials[c]))
                gathered[-1] = follow
            else:
                partials.append(mlp(gathered[-1], w_gate, w_up, w_down))
                sent[-1], partials[c] = barrier((sent[-1], partials[c]))
            done = finish(partials[c], mids[c], gain[3])
            mids[c] = done
            sent.append(gather(send_of(done)))
        return mids, sent

    def device_fn(x_loc, pos_loc, gains, w_q, w_k, w_v, w_o, w_gate, w_up, w_down):
        tp_idx = lax.axis_index('tp')
        sp_idx = lax.axis_index('sp')
        tokens, width = x_loc.shape
        rows = tokens // CHUNKS
        part = rows // tp_size
        heads_tp, dim = w_q.shape[2:]
        kv_tp = w_k.shape[2]
        repeat = sp_size // kv_tp
        w_o = barrier(w_o.reshape(w_o.shape[0], heads_tp * dim, width))

        tables = rope_tables(pos_loc, dim // 2, LOCAL_BASE)
        u_norm = rms_norm(x_loc, gains[0, 0]).astype(BF16)
        qkv = project(u_norm, pack_weights(w_q, w_k, w_v, 0), tables, heads_tp + kv_tp)
        kv = qkv[heads_tp:]
        tail = kv[:, tokens - WINDOW:]
        halo = lax.ppermute(tail, 'sp', [(i, i + 1) for i in range(sp_size - 1)])
        first = jnp.where(sp_idx == 0, WINDOW, 0).astype(jnp.int32).reshape(1)
        attn = local_attention(first, qkv, jnp.concatenate([halo, kv], axis=1), kv_tp)
        residuals = [lax.dynamic_slice_in_dim(x_loc, c * rows + tp_idx * part, part, 0) for c in range(CHUNKS)]
        hidden, u_next = after_attention(
            lambda c: jnp.dot(attn[c * rows:(c + 1) * rows], w_o[0], preferred_element_type=F32),
            residuals, gains[0], w_gate[0], w_up[0], w_down[0], lambda done: rms_norm(done, gains[1, 0]).astype(BF16))

        pairs = tail.reshape(2, kv_tp, WINDOW, dim)
        held = pairs[:, kv_tp - 1]
        for h in range(kv_tp - 1):
            owner = (h + 1) * repeat - 1
            held = jnp.where(sp_idx == owner, lax.ppermute(pairs[:, h], 'sp', [(sp_size - 1, owner)]), held)
        reach = repeat
        while reach > 1:
            moves = [(end - 1, end - 1 - reach // 2) for end in range(reach, sp_size + 1, reach)]
            moved = lax.ppermute(held, 'sp', moves)
            takes = (sp_idx + 1) % reach == reach // 2
            held = jnp.where(takes, moved, held)
            reach //= 2
        k_local = held[0][:, None, :]
        v_local = held[1][:, None, :]

        tables = rope_tables(pos_loc, dim // 2, GLOBAL_BASE)
        packed = pack_weights(w_q, w_k, w_v, 1)
        got = []
        for c in range(CHUNKS):
            qkv = project(u_next[c], packed, tables[:, c * rows:(c + 1) * rows], heads_tp + kv_tp)
            outgoing = jnp.stack([qkv[:heads_tp], jnp.repeat(qkv[heads_tp:heads_tp + kv_tp], repeat, axis=0),
                                  jnp.repeat(qkv[heads_tp + kv_tp:], repeat, axis=0)], axis=1)
            got.append(lax.all_to_all(outgoing, 'sp', 0, 0, tiled=True))
        k_all = jnp.concatenate([g[:, 1] for g in got], axis=1).reshape(sp_size * tokens, dim)
        v_all = jnp.concatenate([g[:, 2] for g in got], axis=1).reshape(sp_size * tokens, dim)

        def global_partial(c):
            back = lax.all_to_all(global_attention(got[c], k_all, v_all, c), 'sp', 0, 0, tiled=True)
            back = back.transpose(1, 0, 2).reshape(rows, heads_tp * dim)
            return jnp.dot(back, w_o[1], preferred_element_type=F32)

        _, outs = after_attention(global_partial, hidden, gains[1], w_gate[1], w_up[1], w_down[1], lambda done: done)
        return jnp.concatenate(outs, axis=0), k_local, v_local, k_all[:, None, :], v_all[:, None, :]

    token_spec = P(('rep', 'sp'), None)
    cache_spec = P('rep', ('tp', 'sp'), None)
    in_specs = (token_spec, P(('rep', 'sp')), P(), P(None, None, 'tp', None), P(None, None, 'tp', None),
                P(None, None, 'tp', None), P(None, 'tp', None, None), P(None, None, 'tp'), P(None, None, 'tp'),
                P(None, 'tp', None))
    out_specs = (token_spec, cache_spec, cache_spec, cache_spec, cache_spec)
    return jax.shard_map(device_fn, mesh=mesh, in_specs=in_specs, out_specs=out_specs, check_vma=False)
```

time: 1720 us -> 1090 us (0.63)
  waiting for transfers between devices: 979 us -> 520 us
  Pallas kernels: 0 us -> 124 us
  local copies, waits for them, and re-layouts: 150 us -> 31 us
  matrix products: 381 us -> 272 us
  loops' own time: 32.6 us -> 0 us
  other arithmetic: 87.6 us -> 64.4 us
    psum x4 -> x0, waiting for transfers between devices: 871 us -> none  [the longest x2 444 us: layer(): lax.psum(jnp.einsum('the,hed->td', attn_back, w_o, preferred_element_type...]
    reduce_scatter x0 -> x8, waiting for transfers between devices: none -> 416 us  [finish(): summed = lax.psum_scatter(partial, 'tp', scatter_dimension=0, tiled=True)]
    pallas_call x0 -> x8, Pallas kernels: none -> 124 us  [the longest x2 57 us: global_attention(): pl.pallas_call(functools.partial(global_kernel, scale2, chunk, total // s...]
    dot_general x106 -> x16, matrix products: 353 us -> 272 us  [the longest x4 80 us: mlp(): up_pre = jnp.dot(u_mlp, w_up, preferred_element_type=F32)]
    all_to_all x2, waiting for transfers between devices: 109 us -> 38.4 us  [device_fn(): got.append(lax.all_to_all(outgoing, 'sp', 0, 0, tiled=True))]
    all_gather x0 -> x8, waiting for transfers between devices: none -> 44 us  [gather(): return lax.all_gather(rows, 'tp', axis=0, tiled=True)]
    another operation x2 -> x0, loops' own time: 32.6 us -> none  [attend(): blocks = lax.map(one_block, jnp.arange(q_heads.shape[0] // Q_BLOCK))]
    unnamed x54 -> x56, local copies, waits for them, and re-layouts: 51.1 us -> 18.7 us
  transfers between devices with their start and end apart: 6 -> 22, of which waited for: 6 -> 16; matrix products, arithmetic and copies ran while one was open for 1% -> 25% of each run, Pallas kernels for 0% -> 5%
where the time goes in v1:
time: 1090 us; the launch traced here: 1080 us
  waiting for transfers between devices  520 us (48%)
  matrix products  272 us (25%)
  Pallas kernels  124 us (11%)
  other arithmetic  64.4 us (6%)
  blocking collectives  33.9 us (3%)
  local copies, waits for them, and re-layouts  31 us (3%)
  starting transfers between devices  21.3 us (2%)
  between operations  15 us (1%)
    reduce_scatter x8, waiting for transfers between devices, finish(): summed = lax.psum_scatter(partial, 'tp', scatter_dimension=0, tiled=True)  416 us
    dot_general x4, matrix products, mlp(): up_pre = jnp.dot(u_mlp, w_up, preferred_element_type=F32)  80 us
    dot_general x4, matrix products, mlp(): gate_pre = jnp.dot(u_mlp, w_gate, preferred_element_type=F32)  77.6 us
    dot_general x4, matrix products, mlp(): return jnp.dot(hidden_act, w_down, preferred_element_type=F32)  77.3 us
    pallas_call x2, Pallas kernels, global_attention(): pl.pallas_call(functools.partial(global_kernel, scale2, chunk, total // s...  57 us
    all_gather x8, waiting for transfers between devices, gather(): return lax.all_gather(rows, 'tp', axis=0, tiled=True)  44 us
    all_to_all x2, waiting for transfers between devices, device_fn(): got.append(lax.all_to_all(outgoing, 'sp', 0, 0, tiled=True))  38.4 us
    all_to_all x2, blocking collectives, global_partial(): lax.all_to_all(global_attention(got[c], k_all, v_all, c), 'sp', 0, 0, til...  33.9 us
  transfers between devices with their start and end apart: 22, of which 16 were waited for; matrix products, arithmetic and copies ran while one was open for 25% of the time, Pallas kernels for 5%

profile of v1, /device:TPU:97, one launch (start us, length us, event | category | flops | bytes accessed | tf_op | source)
XLA Modules:
  0.0 1080.4 jit_solution(17257682584760943100)
XLA Ops:
  8.0 2.0 fusion.121
  9.9 4.1 fusion.36
  14.0 4.0 fusion.108
  18.4 5.5 fusion.38.u_ref
  23.9 9.8 pack_weights.2.w_ref
  33.7 13.7 %project.3.q_ref = bf16[12,768,128]{2,1,0:T(8,128)(2,1)S(1)} custom-call(bf16[768,4096]{1,0:T(8,128)(2,1)S(1)} %fusion.38.u_ref, bf16[4096,1536]{1,0:T(8,128)(2,1)} %pack_weights.2.w_ref, f32[2,768,128]{2,1,0:T(8,128)S(1)} %pad_maximum_fusion.6.table_ref), custom_call_target="tpu_custom_call" | custom-call | flops 9663676416 | bytes 18874368 | tf_op jit(solution)/shard_map/project/pallas_call | solution.py:83
  48.3 4.6 collective-permute-start
  53.0 6.0 collective-permute-done
  60.1 14.2 %local_attention.1 = bf16[768,1024]{1,0:T(8,128)(2,1)S(1)} custom-call(s32[1]{0:T(128)} %bitcast.first_ref, bf16[12,768,128]{2,1,0:T(8,128)(2,1)S(1)} %project.3.q_ref, bf16[4,1280,128]{2,1,0:T(8,128)(2,1)S(1)} %pad_maximum_fusion.5.k_ref.v_ref, bf16[4,1280,128]{2,1,0:T(8,128)(2,1)S(1)} %pad_maximum_fusion.5.k_ref.v_ref), custom_call_target="tpu_custom_call" | custom-call | flops 2415919104 | bytes 6291456 | tf_op jit(solution)/shard_map/local_attention/pallas_call | solution.py:122
  75.5 8.7 fusion.40
  84.3 65.1 %reduce-scatter.9.cloned.1.call-done = f32[96,4096]{1,0:T(8,128)} async-done(((f32[384,4096]{1,0:T(8,128)}), f32[96,4096]{1,0:T(8,128)}) %reduce-scatter.9.cloned.1.call-update) | async-done | bytes 1572880 | tf_op jit(solution)/shard_map/reduce_scatter | solution.py:197
  151.0 2.2 fusion.79
  154.8 8.7 fusion.39
  163.4 27.6 %all-gather.9.cloned.1.call-done = bf16[384,4096]{1,0:T(8,128)(2,1)} async-done(((bf16[96,4096]{1,0:T(8,128)(2,1)}), bf16[384,4096]{1,0:T(8,128)(2,1)}) %all-gather.9.cloned.1.call-update) | async-done | bytes 3145744 | tf_op jit(solution)/shard_map/all_gather | solution.py:194
  191.1 19.4 %fusion.22 = f32[384,3584]{1,0:T(8,128)} fusion(bf16[384,4096]{1,0:T(8,128)(2,1)} %all-gather.9.cloned.1.call-done, bf16[2,4096,3584]{2,1,0:T(8,128)(2,1)} %param.17), kind=kOutput, calls=%fused_computation.22 | convolution fusion | flops 11274289152 | bytes 38010880 | tf_op jit(solution)/shard_map/dot_general | solution.py:201
  210.6 45.1 %reduce-scatter.11.cloned.1.call-done = f32[96,4096]{1,0:T(8,128)} async-done(((f32[384,4096]{1,0:T(8,128)}), f32[96,4096]{1,0:T(8,128)}) %reduce-scatter.11.cloned.1.call-update) | async-done | bytes 1572880 | tf_op jit(solution)/shard_map/reduce_scatter | solution.py:197
  257.3 2.1 fusion.83
  260.9 20.1 %fusion.64.clone.2 = bf16[384,3584]{1,0:T(8,128)(2,1)} fusion(bf16[384,4096]{1,0:T(8,128)(2,1)} %all-gather.9.cloned.1.call-done, bf16[2,4096,3584]{2,1,0:T(8,128)(2,1)} %param.18, f32[384,3584]{1,0:T(8,128)} %fusion.22), kind=kOutput, calls=%fused_computation.55.clone.clone.clone | convolution fusion | flops 11282546688 | bytes 40763392 | tf_op jit(solution)/shard_map/dot_general | solution.py:202
  281.1 19.4 %fusion.14 = f32[384,4096]{1,0:T(8,128)} fusion(bf16[2,3584,4096]{2,1,0:T(8,128)(2,1)} %param.19, bf16[384,3584]{1,0:T(8,128)(2,1)} %fusion.64.clone.2), kind=kOutput, calls=%fused_computation.14 | convolution fusion | flops 11274289152 | bytes 38404096 | tf_op jit(solution)/shard_map/dot_general | solution.py:204
  301.0 19.4 %fusion.20 = f32[384,3584]{1,0:T(8,128)} fusion(bf16[384,4096]{1,0:T(8,128)(2,1)} %all-gather.11.cloned.1.call-done, bf16[2,4096,3584]{2,1,0:T(8,128)(2,1)} %param.17), kind=kOutput, calls=%fused_computation.20 | convolution fusion | flops 11274289152 | bytes 38010880 | tf_op jit(solution)/shard_map/dot_general | solution.py:201
  320.5 41.3 %reduce-scatter.13.cloned.1.call-done = f32[96,4096]{1,0:T(8,128)} async-done(((f32[384,4096]{1,0:T(8,128)}), f32[96,4096]{1,0:T(8,128)}) %reduce-scatter.13.cloned.1.call-update) | async-done | bytes 1572880 | tf_op jit(solution)/shard_map/reduce_scatter | solution.py:197
  363.4 1.9 fusion.87
  367.7 20.1 %fusion.61.clone.5 = bf16[384,3584]{1,0:T(8,128)(2,1)} fusion(bf16[384,4096]{1,0:T(8,128)(2,1)} %all-gather.11.cloned.1.call-done, bf16[2,4096,3584]{2,1,0:T(8,128)(2,1)} %param.18, f32[384,3584]{1,0:T(8,128)} %fusion.20), kind=kOutput, calls=%fused_computation.54.clone.clone.clone.2 | convolution fusion | flops 11282546688 | bytes 40763392 | tf_op jit(solution)/shard_map/dot_general | solution.py:202
  387.8 19.3 %fusion.12 = f32[384,4096]{1,0:T(8,128)} fusion(bf16[2,3584,4096]{2,1,0:T(8,128)(2,1)} %param.19, bf16[384,3584]{1,0:T(8,128)(2,1)} %fusion.61.clone.5), kind=kOutput, calls=%fused_computation.12 | convolution fusion | flops 11274289152 | bytes 38404096 | tf_op jit(solution)/shard_map/dot_general | solution.py:204
  407.3 61.4 %reduce-scatter.15.cloned.1.call-done = f32[96,4096]{1,0:T(8,128)} async-done(((f32[384,4096]{1,0:T(8,128)}), f32[96,4096]{1,0:T(8,128)}) %reduce-scatter.15.cloned.1.call-update) | async-done | bytes 1572880 | tf_op jit(solution)/shard_map/reduce_scatter | solution.py:197
  470.3 1.9 fusion.91
  473.5 2.2 copy-done.1
  475.6 2.2 copy-done.3
  477.8 9.9 pack_weights.3.w_ref
  489.7 9.5 project.4
  501.3 5.5 all-to-all-start
  506.8 3.2 all-gather.15.cloned.1.call-done.u_ref
  510.0 1.9 copy-done.11
  511.9 9.5 project.5
  523.3 12.1 %all-to-all-done.q_ref = bf16[8,3,384,128]{3,2,1,0:T(8,128)(2,1)S(1)} async-done(((bf16[8,3,384,128]{3,2,1,0:T(8,128)(2,1)}), bf16[8,3,384,128]{3,2,1,0:T(8,128)(2,1)S(1)}, u32[]{:S(2)}, u32[]{:S(2)}) %all-to-all-start) | async-done | bytes 2359328 | tf_op jit(solution)/shard_map/all_to_all | solution.py:275
  536.9 4.7 all-to-all-start.1
  541.6 2.7 slice_bitcast_fusion.7
  544.3 26.2 %all-to-all-done.1.q_ref = bf16[8,3,384,128]{3,2,1,0:T(8,128)(2,1)S(1)} async-done(((bf16[8,3,384,128]{3,2,1,0:T(8,128)(2,1)}), bf16[8,3,384,128]{3,2,1,0:T(8,128)(2,1)S(1)}, u32[]{:S(2)}, u32[]{:S(2)}) %all-to-all-start.1) | async-done | bytes 2359328 | tf_op jit(solution)/shard_map/all_to_all | solution.py:275
  572.0 2.5 copy-done.5
  574.5 27.6 %global_attention.2 = bf16[8,384,128]{2,1,0:T(8,128)(2,1)S(1)} custom-call(bf16[8,3,384,128]{3,2,1,0:T(8,128)(2,1)S(1)} %copy-done.5, bf16[6144,128]{1,0:T(8,128)(2,1)S(1)} %bitcast.166, bf16[6144,128]{1,0:T(8,128)(2,1)S(1)} %bitcast.163), custom_call_target="tpu_custom_call" | custom-call | flops 9663676416 | bytes 6291456 | tf_op jit(solution)/shard_map/global_attention/pallas_call | solution.py:175
  602.1 16.4 %all_to_all.20 = bf16[8,384,128]{2,1,0:T(8,128)(2,1)} all-to-all(bf16[8,384,128]{2,1,0:T(8,128)(2,1)S(1)} %global_attention.2), channel_id=1, replica_groups=mesh['rep'=1,'tp'=4,'sp'=8] {'sp'}, dimensions={0} | all-to-all | bytes 1572864 | tf_op jit(solution)/shard_map/all_to_all | solution.py:280
  618.5 2.3 copy.28
  620.8 9.8 fusion.42
  630.8 59.6 %reduce-scatter.17.cloned.1.call-done = f32[96,4096]{1,0:T(8,128)} async-done(((f32[384,4096]{1,0:T(8,128)}), f32[96,4096]{1,0:T(8,128)}) %reduce-scatter.17.cloned.1.call-update) | async-done | bytes 1572880 | tf_op jit(solution)/shard_map/reduce_scatter | solution.py:197
  692.1 2.1 fusion.95
  699.2 29.4 %global_attention.3 = bf16[8,384,128]{2,1,0:T(8,128)(2,1)S(1)} custom-call(bf16[8,3,384,128]{3,2,1,0:T(8,128)(2,1)S(1)} %all-to-all-done.1.q_ref, bf16[6144,128]{1,0:T(8,128)(2,1)S(1)} %bitcast.168, bf16[6144,128]{1,0:T(8,128)(2,1)S(1)} %bitcast.165), custom_call_target="tpu_custom_call" | custom-call | flops 9663676416 | bytes 6291456 | tf_op jit(solution)/shard_map/global_attention/pallas_call | solution.py:175
  728.6 17.5 %all_to_all.21 = bf16[8,384,128]{2,1,0:T(8,128)(2,1)S(1)} all-to-all(bf16[8,384,128]{2,1,0:T(8,128)(2,1)S(1)} %global_attention.3), channel_id=1, replica_groups=mesh['rep'=1,'tp'=4,'sp'=8] {'sp'}, dimensions={0} | all-to-all | bytes 1572864 | tf_op jit(solution)/shard_map/all_to_all | solution.py:280
  746.5 9.6 fusion.41
  756.2 19.3 %fusion.10 = f32[384,3584]{1,0:T(8,128)} fusion(bf16[384,4096]{1,0:T(8,128)(2,1)} %all-gather.17.cloned.1.call-done, bf16[2,4096,3584]{2,1,0:T(8,128)(2,1)} %param.17), kind=kOutput, calls=%fused_computation.10 | convolution fusion | flops 11274289152 | bytes 38010880 | tf_op jit(solution)/shard_map/dot_general | solution.py:201
  775.6 40.3 %reduce-scatter.19.cloned.1.call-done = f32[96,4096]{1,0:T(8,128)} async-done(((f32[384,4096]{1,0:T(8,128)}), f32[96,4096]{1,0:T(8,128)}) %reduce-scatter.19.cloned.1.call-update) | async-done | bytes 1572880 | tf_op jit(solution)/shard_map/reduce_scatter | solution.py:197
  817.5 1.9 fusion.99
  820.9 19.9 %fusion.58.clone.2 = bf16[384,3584]{1,0:T(8,128)(2,1)} fusion(bf16[384,4096]{1,0:T(8,128)(2,1)} %all-gather.17.cloned.1.call-done, bf16[2,4096,3584]{2,1,0:T(8,128)(2,1)} %param.18, f32[384,3584]{1,0:T(8,128)} %fusion.10), kind=kOutput, calls=%fused_computation.53.clone.clone.clone | convolution fusion | flops 11282546688 | bytes 40763392 | tf_op jit(solution)/shard_map/dot_general | solution.py:202
  840.9 19.3 %fusion.2 = f32[384,4096]{1,0:T(8,128)} fusion(bf16[2,3584,4096]{2,1,0:T(8,128)(2,1)} %param.19, bf16[384,3584]{1,0:T(8,128)(2,1)} %fusion.58.clone.2), kind=kOutput, calls=%fused_computation.2 | convolution fusion | flops 11274289152 | bytes 38404096 | tf_op jit(solution)/shard_map/dot_general | solution.py:204
  860.3 19.4 %fusion.8 = f32[384,3584]{1,0:T(8,128)} fusion(bf16[384,4096]{1,0:T(8,128)(2,1)} %all-gather.19.cloned.1.call-done, bf16[2,4096,3584]{2,1,0:T(8,128)(2,1)} %param.17), kind=kOutput, calls=%fused_computation.8 | convolution fusion | flops 11274289152 | bytes 38010880 | tf_op jit(solution)/shard_map/dot_general | solution.py:201
  879.7 42.2 %reduce-scatter.21.cloned.1.call-done = f32[96,4096]{1,0:T(8,128)} async-done(((f32[384,4096]{1,0:T(8,128)}), f32[96,4096]{1,0:T(8,128)}) %reduce-scatter.21.cloned.1.call-update) | async-done | bytes 1572880 | tf_op jit(solution)/shard_map/reduce_scatter | solution.py:197
  923.5 2.6 fusion.98
  926.5 19.9 %fusion.55.clone.5 = bf16[384,3584]{1,0:T(8,128)(2,1)} fusion(bf16[384,4096]{1,0:T(8,128)(2,1)} %all-gather.19.cloned.1.call-done, bf16[2,4096,3584]{2,1,0:T(8,128)(2,1)} %param.18, f32[384,3584]{1,0:T(8,128)} %fusion.8), kind=kOutput, calls=%fused_computation.52.clone.clone.clone.2 | convolution fusion | flops 11282546688 | bytes 40763392 | tf_op jit(solution)/shard_map/dot_general | solution.py:202
  946.4 19.3 %fusion = f32[384,4096]{1,0:T(8,128)} fusion(bf16[2,3584,4096]{2,1,0:T(8,128)(2,1)} %param.19, bf16[384,3584]{1,0:T(8,128)(2,1)} %fusion.55.clone.5), kind=kOutput, calls=%fused_computation | convolution fusion | flops 11274289152 | bytes 38404096 | tf_op jit(solution)/shard_map/dot_general | solution.py:204
  965.8 61.4 %reduce-scatter.23.cloned.1.call-done = f32[96,4096]{1,0:T(8,128)} async-done(((f32[384,4096]{1,0:T(8,128)}), f32[96,4096]{1,0:T(8,128)}) %reduce-scatter.23.cloned.1.call-update) | async-done | bytes 1572880 | tf_op jit(solution)/shard_map/reduce_scatter | solution.py:197
  1028.9 2.6 fusion.102
  1036.4 12.7 %collective-permute-done.2 = bf16[2,512,128]{2,1,0:T(8,128)(2,1)} collective-permute-done((bf16[2,512,128]{2,1,0:T(8,128)(2,1)S(1)}, bf16[2,512,128]{2,1,0:T(8,128)(2,1)}, u32[]{:S(2)}, u32[]{:S(2)}) %collective-permute-start.2) | collective-permute-done | bytes 262176 | tf_op jit(solution)/shard_map/ppermute | solution.py:261
  1049.0 1.7 broadcast_select_fusion
  1054.9 13.2 %all-gather.23.cloned.1.call-done = bf16[384,4096]{1,0:T(8,128)(2,1)} async-done(((bf16[96,4096]{1,0:T(8,128)(2,1)}), bf16[384,4096]{1,0:T(8,128)(2,1)}) %all-gather.23.cloned.1.call-update) | async-done | bytes 3145744 | tf_op jit(solution)/shard_map/all_gather | solution.py:194
  1068.1 5.3 pad_maximum_fusion
  (152 shorter events, 50.1 us)
Async XLA Ops:
  7.2 142.2 %reduce-scatter.9.cloned.1.call-start = ((), (), s32[]{:S(2)}) async-start(), calls=%async_computation.12 | async-start | bytes 7864320 | tf_op jit(solution)/shard_map/reduce_scatter | solution.py:197
  18.3 5.5 copy-start
  18.3 5.5 copy-start.2
  48.3 10.7 collective-permute-start
  74.3 1.1 copy-start.12
  84.2 106.8 %all-gather.9.cloned.1.call-start = ((), (), s32[]{:S(2)}) async-start(), calls=%async_computation.13 | async-start | bytes 3932160 | tf_op jit(solution)/shard_map/all_gather | solution.py:194
  151.0 3.8 copy-start.13
  154.5 101.2 %reduce-scatter.11.cloned.1.call-start = ((), (), s32[]{:S(2)}) async-start(), calls=%async_computation.14 | async-start | bytes 7864320 | tf_op jit(solution)/shard_map/reduce_scatter | solution.py:197
  191.1 109.4 %all-gather.11.cloned.1.call-start = ((), (), s32[]{:S(2)}) async-start(), calls=%async_computation.15 | async-start | bytes 3932160 | tf_op jit(solution)/shard_map/all_gather | solution.py:194
  260.6 101.2 %reduce-scatter.13.cloned.1.call-start = ((), (), s32[]{:S(2)}) async-start(), calls=%async_computation.16 | async-start | bytes 7864320 | tf_op jit(solution)/shard_map/reduce_scatter | solution.py:197
  300.5 62.9 %copy-start.27 = (f32[1,1,4096]{2,1,0:T(1,128)S(1)}, f32[1,1,4096]{2,1,0:T(1,128)}, u32[]{:S(2)}) copy-start(f32[1,1,4096]{2,1,0:T(1,128)} %get-tuple-element.56) | copy-start | bytes 49156
  300.5 106.6 %all-gather.13.cloned.1.call-start = ((), (), s32[]{:S(2)}) async-start(), calls=%async_computation.17 | async-start | bytes 3932160 | tf_op jit(solution)/shard_map/all_gather | solution.py:194
  320.5 45.8 %copy-start.26 = (f32[1,1,4096]{2,1,0:T(1,128)S(1)}, f32[1,1,4096]{2,1,0:T(1,128)}, u32[]{:S(2)}) copy-start(f32[1,1,4096]{2,1,0:T(1,128)} %get-tuple-element.55) | copy-start | bytes 49156
  365.4 0.9 copy-start.14
  367.5 101.2 %reduce-scatter.15.cloned.1.call-start = ((), (), s32[]{:S(2)}) async-start(), calls=%async_computation.18 | async-start | bytes 7864320 | tf_op jit(solution)/shard_map/reduce_scatter | solution.py:197
  407.2 102.8 %all-gather.15.cloned.1.call-start = ((), (), s32[]{:S(2)}) async-start(), calls=%async_computation.19 | async-start | bytes 3932160 | tf_op jit(solution)/shard_map/all_gather | solution.py:194
  473.5 2.2 copy-start.1
  475.6 2.2 copy-start.3
  477.8 9.9 copy-start.20
  477.8 9.9 copy-start.21
  477.8 9.9 copy-start.22
  487.8 1.9 copy-start.10
  501.3 34.2 %all-to-all-start = ((bf16[8,3,384,128]{3,2,1,0:T(8,128)(2,1)}), bf16[8,3,384,128]{3,2,1,0:T(8,128)(2,1)S(1)}, u32[]{:S(2)}, u32[]{:S(2)}) async-start(bf16[8,3,384,128]{3,2,1,0:T(8,128)(2,1)} %copy.25), calls=%async_computation.3 | async-start | bytes 4718592 | tf_op jit(solution)/shard_map/all_to_all | solution.py:275
  510.0 1.9 copy-start.11
  535.5 1.4 copy-start.4
  536.9 33.6 %all-to-all-start.1 = ((bf16[8,3,384,128]{3,2,1,0:T(8,128)(2,1)}), bf16[8,3,384,128]{3,2,1,0:T(8,128)(2,1)S(1)}, u32[]{:S(2)}, u32[]{:S(2)}) async-start(bf16[8,3,384,128]{3,2,1,0:T(8,128)(2,1)} %pad_maximum_fusion.2), calls=%async_computation.5 | async-start | bytes 4718592 | tf_op jit(solution)/shard_map/all_to_all | solution.py:275
  541.6 148.8 %reduce-scatter.17.cloned.1.call-start = ((), (), s32[]{:S(2)}) async-start(), calls=%async_computation.20 | async-start | bytes 7864320 | tf_op jit(solution)/shard_map/reduce_scatter | solution.py:197
  570.5 1.1 copy-start.19
  570.5 1.4 copy-start.18
  571.7 2.9 copy-start.5
  571.8 30.3 %copy-start.6 = (bf16[8,768,128]{2,1,0:T(8,128)(2,1)}, bf16[8,768,128]{2,1,0:T(8,128)(2,1)S(1)}, u32[]{:S(2)}) copy-start(bf16[8,768,128]{2,1,0:T(8,128)(2,1)S(1)} %pad_maximum_fusion.4) | copy-start | bytes 4718596
  572.0 30.1 %copy-start.8 = (bf16[8,768,128]{2,1,0:T(8,128)(2,1)}, bf16[8,768,128]{2,1,0:T(8,128)(2,1)S(1)}, u32[]{:S(2)}) copy-start(bf16[8,768,128]{2,1,0:T(8,128)(2,1)S(1)} %pad_maximum_fusion.3) | copy-start | bytes 4718596
  630.7 61.4 %copy-start.25 = (f32[1,1,4096]{2,1,0:T(1,128)S(1)}, f32[1,1,4096]{2,1,0:T(1,128)}, u32[]{:S(2)}) copy-start(f32[1,1,4096]{2,1,0:T(1,128)} %get-tuple-element.54) | copy-start | bytes 49156
  630.7 64.4 %copy-start.24 = (f32[1,1,4096]{2,1,0:T(1,128)S(1)}, f32[1,1,4096]{2,1,0:T(1,128)}, u32[]{:S(2)}) copy-start(f32[1,1,4096]{2,1,0:T(1,128)} %get-tuple-element.60) | copy-start | bytes 49156
  630.7 125.4 %all-gather.17.cloned.1.call-start = ((), (), s32[]{:S(2)}) async-start(), calls=%async_computation.21 | async-start | bytes 3932160 | tf_op jit(solution)/shard_map/all_gather | solution.py:194
  694.2 0.9 copy-start.15
  696.3 119.6 %reduce-scatter.19.cloned.1.call-start = ((), (), s32[]{:S(2)}) async-start(), calls=%async_computation.22 | async-start | bytes 7864320 | tf_op jit(solution)/shard_map/reduce_scatter | solution.py:197
  696.4 1.4 copy-start.7
  697.8 1.4 copy-start.9
  756.2 104.0 %all-gather.19.cloned.1.call-start = ((), (), s32[]{:S(2)}) async-start(), calls=%async_computation.23 | async-start | bytes 3932160 | tf_op jit(solution)/shard_map/all_gather | solution.py:194
  820.7 101.2 %reduce-scatter.21.cloned.1.call-start = ((), (), s32[]{:S(2)}) async-start(), calls=%async_computation.24 | async-start | bytes 7864320 | tf_op jit(solution)/shard_map/reduce_scatter | solution.py:197
  860.2 63.3 %copy-start.16 = (bf16[96,4096]{1,0:T(8,128)(2,1)S(1)}, bf16[96,4096]{1,0:T(8,128)(2,1)}, u32[]{:S(2)}) copy-start(bf16[96,4096]{1,0:T(8,128)(2,1)} %copy-done.15) | copy-start | bytes 2359300
  860.2 63.3 %copy-start.23 = (f32[1,1,4096]{2,1,0:T(1,128)S(1)}, f32[1,1,4096]{2,1,0:T(1,128)}, u32[]{:S(2)}) copy-start(f32[1,1,4096]{2,1,0:T(1,128)} %get-tuple-element.53) | copy-start | bytes 49156
  860.2 105.4 %all-gather.21.cloned.1.call-start = ((), (), s32[]{:S(2)}) async-start(), calls=%async_computation.25 | async-start | bytes 3932160 | tf_op jit(solution)/shard_map/all_gather | solution.py:194
  926.2 101.0 %reduce-scatter.23.cloned.1.call-start = ((), (), s32[]{:S(2)}) async-start(), calls=%async_computation.26 | async-start | bytes 7864320 | tf_op jit(solution)/shard_map/reduce_scatter | solution.py:197
  965.8 102.3 %all-gather.23.cloned.1.call-start = ((), (), s32[]{:S(2)}) async-start(), calls=%async_computation.27 | async-start | bytes 3932160 | tf_op jit(solution)/shard_map/all_gather | solution.py:194
  1031.5 36.6 %copy-start.17 = (bf16[384,4096]{1,0:T(8,128)(2,1)S(1)}, bf16[384,4096]{1,0:T(8,128)(2,1)}, u32[]{:S(2)}) copy-start(bf16[384,4096]{1,0:T(8,128)(2,1)} %all-gather.21.cloned.1.call-done) | copy-start | bytes 9437188
  1032.7 1.4 collective-permute-start.1
  1035.0 14.0 %collective-permute-start.2 = (bf16[2,512,128]{2,1,0:T(8,128)(2,1)S(1)}, bf16[2,512,128]{2,1,0:T(8,128)(2,1)}, u32[]{:S(2)}, u32[]{:S(2)}) collective-permute-start(bf16[2,512,128]{2,1,0:T(8,128)(2,1)S(1)} %fusion.106), channel_id=1, source_target_pairs={{3,1},{7,5},{11,9},{15,13},{19,17},{23,21},{27,25},{31,29}} | collective-permute-start | bytes 786440 | tf_op jit(solution)/shard_map/ppermute | solution.py:261
  1050.7 2.4 collective-permute-start.3
Sparse Core Ops, SparseCore 0:
  84.3 64.9 reduce-scatter.8
  154.6 36.3 all-gather.8
  193.9 61.7 reduce-scatter.10
  260.7 36.3 all-gather.10
  300.6 61.1 reduce-scatter.12
  367.6 36.3 all-gather.12
  407.3 61.3 reduce-scatter.14
  473.6 36.3 all-gather.14
  630.9 59.5 reduce-scatter.16
  696.4 36.3 all-gather.16
  756.3 59.5 reduce-scatter.18
  820.8 36.3 all-gather.18
  860.3 61.5 reduce-scatter.20
  926.3 36.3 all-gather.20
  965.9 61.3 reduce-scatter.22
  1031.7 36.3 all-gather.22

commit v2 on v1

--- a/solution.py
+++ b/solution.py
@@ -8,9 +8,9 @@
 from jax.experimental.pallas import tpu as pltpu
 from jax.sharding import PartitionSpec as P
 
+
 NORM_EPS = 1e-6
 WINDOW = 512
-Q_BLOCK = 256
 LOCAL_BASE = 10000.0
 GLOBAL_BASE = 1000000.0
 CHUNKS = 2
@@ -93,10 +93,10 @@
     )(u_norm, packed, tables)
 
 
-def local_kernel(scale2, first_ref, q_ref, k_ref, v_ref, out_ref):
+def local_kernel(scale2, chunk, first_ref, q_ref, k_ref, v_ref, out_ref):
     heads, rows, dim = q_ref.shape
     span = rows + WINDOW
-    start = pl.multiple_of(pl.program_id(1) * rows, rows)
+    start = chunk * rows
     k_tile = k_ref[0, pl.ds(start, span), :]
     v_tile = v_ref[0, pl.ds(start, span), :]
     q_idx = lax.broadcasted_iota(jnp.int32, (rows, span), 0)
@@ -112,22 +112,23 @@
         out_ref[:, head * dim:(head + 1) * dim] = out.astype(BF16)
 
 
-def local_attention(first, qkv, kv_ext, kv_heads):
+def local_attention(first, qkv, kv_ext, kv_heads, chunk):
     tokens, dim = qkv.shape[1:]
+    rows = tokens // CHUNKS
     q_heads = qkv.shape[0] - 2 * kv_heads
     group = q_heads // kv_heads
     scale2 = dim ** -0.5 * math.log2(math.e)
-    k_spec = pl.BlockSpec((1, WINDOW + tokens, dim), lambda h, i: (h, 0, 0))
-    v_spec = pl.BlockSpec((1, WINDOW + tokens, dim), lambda h, i: (kv_heads + h, 0, 0))
+    k_spec = pl.BlockSpec((1, WINDOW + tokens, dim), lambda h: (h, 0, 0))
+    v_spec = pl.BlockSpec((1, WINDOW + tokens, dim), lambda h: (kv_heads + h, 0, 0))
     return pl.pallas_call(
-        functools.partial(local_kernel, scale2),
-        grid=(kv_heads, tokens // Q_BLOCK),
-        in_specs=[pl.BlockSpec(memory_space=pltpu.SMEM), pl.BlockSpec((group, Q_BLOCK, dim), lambda h, i: (h, i, 0)),
+        functools.partial(local_kernel, scale2, chunk),
+        grid=(kv_heads,),
+        in_specs=[pl.BlockSpec(memory_space=pltpu.SMEM), pl.BlockSpec((group, rows, dim), lambda h: (h, chunk, 0)),
                   k_spec, v_spec],
-        out_specs=pl.BlockSpec((Q_BLOCK, group * dim), lambda h, i: (i, h)),
-        out_shape=jax.ShapeDtypeStruct((tokens, q_heads * dim), BF16),
+        out_specs=pl.BlockSpec((rows, group * dim), lambda h: (0, h)),
+        out_shape=jax.ShapeDtypeStruct((rows, q_heads * dim), BF16),
         compiler_params=pltpu.CompilerParams(vmem_limit_bytes=40 << 20),
-        cost_estimate=pl.CostEstimate(flops=4 * tokens * q_heads * dim * (WINDOW + Q_BLOCK), bytes_accessed=8 * tokens * q_heads * dim,
+        cost_estimate=pl.CostEstimate(flops=4 * rows * q_heads * dim * (WINDOW + rows), bytes_accessed=8 * rows * q_heads * dim,
                                       transcendentals=0),
         name='local_attention',
     )(first, qkv, kv_ext, kv_ext)
@@ -161,7 +162,7 @@
         at = pl.multiple_of(j * k_block, k_block)
         return step(carry, k_ref[pl.ds(at, k_block), :], v_ref[pl.ds(at, k_block), :], None)
 
-    top, total, acc = lax.fori_loop(0, shard, full, carry)
+    _, total, acc = lax.fori_loop(0, shard, full, carry)
     out_ref[0] = (acc / total).astype(BF16)
 
 
@@ -193,8 +194,33 @@
     def gather(rows):
         return lax.all_gather(rows, 'tp', axis=0, tiled=True)
 
-    def finish(partial, residual, gain):
+    def ring_gather(block):
+        me = lax.axis_index('tp')
+        up = [(i, (i + 1) % tp_size) for i in range(tp_size)]
+        down = [(i, (i - 1) % tp_size) for i in range(tp_size)]
+        size = block.shape[0]
+        whole = jnp.zeros((tp_size * size, block.shape[1]), block.dtype)
+
+        def put(whole, value, owner, at=0):
+            return lax.dynamic_update_slice_in_dim(whole, value, (owner % tp_size) * size + at, 0)
+
+        whole = put(whole, block, me)
+        left = lax.ppermute(block, 'tp', up)
+        right = lax.ppermute(block, 'tp', down)
+        far_left = lax.ppermute(left[:size // 2], 'tp', up)
+        far_right = lax.ppermute(right[size // 2:], 'tp', down)
+        whole = put(whole, left, me + tp_size - 1)
+        whole = put(whole, right, me + 1)
+        whole = put(whole, far_left, me + 2)
+        return put(whole, far_right, me + 2, size // 2)
+
+    def gather_of(ringed):
+        return ring_gather if ringed and tp_size == 4 else gather
+
+    def finish(partial, residual, gain, ahead):
         summed = lax.psum_scatter(partial, 'tp', scatter_dimension=0, tiled=True)
+        if ahead is not None:
+            summed, _ = barrier((summed, ahead))
         return (residual.astype(F32) + rms_norm(summed, gain)).astype(BF16)
 
     def mlp(u_mlp, w_gate, w_up, w_down):
@@ -203,16 +229,18 @@
         hidden_act = (jax.nn.silu(gate_pre) * up_pre).astype(BF16)
         return jnp.dot(hidden_act, w_down, preferred_element_type=F32)
 
-    def after_attention(partial_of, residuals, gain, w_gate, w_up, w_down, send_of):
+    def after_attention(partial_of, residuals, gain, w_gate, w_up, w_down, send_of, ring_sent):
         mids, gathered, partials, sent = [], [], [], []
+        ahead = None
         for c in range(CHUNKS):
             o_partial = partial_of(c)
             if c > 0:
-                gathered[-1], o_partial = barrier((gathered[-1], o_partial))
                 partials.append(mlp(gathered[-1], w_gate, w_up, w_down))
-            x_mid = finish(o_partial, residuals[c], gain[1])
+            x_mid = finish(o_partial, residuals[c], gain[1], ahead)
             mids.append(x_mid)
-            gathered.append(gather(rms_norm(x_mid, gain[2]).astype(BF16)))
+            ahead = rms_norm(x_mid, gain[2]).astype(BF16)
+            gathered.append(gather_of(c == 0)(ahead))
+        ahead = None
         for c in range(CHUNKS):
             if c + 1 < CHUNKS:
                 follow = gathered[-1]
@@ -220,10 +248,12 @@
                 gathered[-1] = follow
             else:
                 partials.append(mlp(gathered[-1], w_gate, w_up, w_down))
-                sent[-1], partials[c] = barrier((sent[-1], partials[c]))
-            done = finish(partials[c], mids[c], gain[3])
+                if not ring_sent:
+                    sent[-1], partials[c] = barrier((sent[-1], partials[c]))
+            done = finish(partials[c], mids[c], gain[3], ahead)
             mids[c] = done
-            sent.append(gather(send_of(done)))
+            ahead = send_of(done)
+            sent.append(gather_of(c == 0 and ring_sent)(ahead))
         return mids, sent
 
     def device_fn(x_loc, pos_loc, gains, w_q, w_k, w_v, w_o, w_gate, w_up, w_down):
@@ -244,11 +274,11 @@
         tail = kv[:, tokens - WINDOW:]
         halo = lax.ppermute(tail, 'sp', [(i, i + 1) for i in range(sp_size - 1)])
         first = jnp.where(sp_idx == 0, WINDOW, 0).astype(jnp.int32).reshape(1)
-        attn = local_attention(first, qkv, jnp.concatenate([halo, kv], axis=1), kv_tp)
+        kv_ext = jnp.concatenate([halo, kv], axis=1)
         residuals = [lax.dynamic_slice_in_dim(x_loc, c * rows + tp_idx * part, part, 0) for c in range(CHUNKS)]
         hidden, u_next = after_attention(
-            lambda c: jnp.dot(attn[c * rows:(c + 1) * rows], w_o[0], preferred_element_type=F32),
-            residuals, gains[0], w_gate[0], w_up[0], w_down[0], lambda done: rms_norm(done, gains[1, 0]).astype(BF16))
+            lambda c: jnp.dot(local_attention(first, qkv, kv_ext, kv_tp, c), w_o[0], preferred_element_type=F32),
+            residuals, gains[0], w_gate[0], w_up[0], w_down[0], lambda done: rms_norm(done, gains[1, 0]).astype(BF16), True)
 
         pairs = tail.reshape(2, kv_tp, WINDOW, dim)
         held = pairs[:, kv_tp - 1]
@@ -281,7 +311,7 @@
             back = back.transpose(1, 0, 2).reshape(rows, heads_tp * dim)
             return jnp.dot(back, w_o[1], preferred_element_type=F32)
 
-        _, outs = after_attention(global_partial, hidden, gains[1], w_gate[1], w_up[1], w_down[1], lambda done: done)
+        _, outs = after_attention(global_partial, hidden, gains[1], w_gate[1], w_up[1], w_down[1], lambda done: done, False)
         return jnp.concatenate(outs, axis=0), k_local, v_local, k_all[:, None, :], v_all[:, None, :]
 
     token_spec = P(('rep', 'sp'), None)

time: 1090 us -> 1070 us (0.982)
  waiting for transfers between devices: 520 us -> 485 us
  starting transfers between devices: 21.3 us -> 42.4 us
    reduce_scatter x8, waiting for transfers between devices: 416 us -> 366 us  [finish(): summed = lax.psum_scatter(partial, 'tp', scatter_dimension=0, tiled=True)]
    ppermute x0 -> x12, waiting for transfers between devices: none -> 43.2 us  [the longest x3 26.8 us: ring_gather(): far_left = lax.ppermute(left[:size // 2], 'tp', up)]
    all_gather x8 -> x5, waiting for transfers between devices: 44 us -> 13.1 us  [gather(): return lax.all_gather(rows, 'tp', axis=0, tiled=True)]
    ppermute x0 -> x12, starting transfers between devices: none -> 18 us  [the longest x3 9.36 us: ring_gather(): far_right = lax.ppermute(right[size // 2:], 'tp', down)]
  transfers between devices with their start and end apart: 22 -> 31, of which waited for: 16 -> 22; matrix products, arithmetic and copies ran while one was open for 25% -> 28% of each run, Pallas kernels for 5% -> 6%
where the time goes in v2:
time: 1070 us
  waiting for transfers between devices  485 us (45%)
  matrix products  271 us (25%)
  Pallas kernels  124 us (12%)
  other arithmetic  60.4 us (6%)
  starting transfers between devices  42.4 us (4%)
  local copies, waits for them, and re-layouts  37.7 us (4%)
  blocking collectives  31.2 us (3%)
  between operations  15.3 us (1%)
    reduce_scatter x8, waiting for transfers between devices, finish(): summed = lax.psum_scatter(partial, 'tp', scatter_dimension=0, tiled=True)  366 us
    dot_general x4, matrix products, mlp(): return jnp.dot(hidden_act, w_down, preferred_element_type=F32)  78 us
    dot_general x4, matrix products, mlp(): gate_pre = jnp.dot(u_mlp, w_gate, preferred_element_type=F32)  77.6 us
    dot_general x4, matrix products, mlp(): up_pre = jnp.dot(u_mlp, w_up, preferred_element_type=F32)  77.4 us
    pallas_call x2, Pallas kernels, global_attention(): pl.pallas_call(functools.partial(global_kernel, scale2, chunk, total // s...  58.3 us
    all_to_all x2, waiting for transfers between devices, device_fn(): got.append(lax.all_to_all(outgoing, 'sp', 0, 0, tiled=True))  43.9 us
    pallas_call x3, Pallas kernels, project(): pl.pallas_call(functools.partial(project_kernel, rotated_heads // step, d...  32.6 us
    all_to_all x2, blocking collectives, global_partial(): lax.all_to_all(global_attention(got[c], k_all, v_all, c), 'sp', 0, 0, til...  31.2 us
  transfers between devices with their start and end apart: 31, of which 22 were waited for; matrix products, arithmetic and copies ran while one was open for 28% of the time, Pallas kernels for 6%

profile of v2, /device:TPU:97, one launch (start us, length us, event | category | flops | bytes accessed | tf_op | source)
XLA Modules:
  0.0 1066.7 jit_solution(9270543125474143066)
XLA Ops:
  9.3 4.2 fusion.36
  13.9 2.8 fusion.38.u_ref
  16.7 4.1 multiply_cosine_fusion
  21.1 9.9 pack_weights.2.w_ref
  31.0 13.6 %project.3.q_ref = bf16[12,768,128]{2,1,0:T(8,128)(2,1)S(1)} custom-call(bf16[768,4096]{1,0:T(8,128)(2,1)S(1)} %fusion.38.u_ref, bf16[4096,1536]{1,0:T(8,128)(2,1)} %pack_weights.2.w_ref, f32[2,768,128]{2,1,0:T(8,128)S(1)} %pad_maximum_fusion.6.table_ref), custom_call_target="tpu_custom_call" | custom-call | flops 9663676416 | bytes 18874368 | tf_op jit(solution)/shard_map/project/pallas_call | solution.py:83
  44.7 4.8 collective-permute-start
  50.9 4.4 collective-permute-done
  55.5 6.6 local_attention.2
  62.0 8.7 fusion.40
  72.5 6.6 local_attention.3
  79.1 9.8 fusion.39
  89.1 47.0 %reduce-scatter.9.cloned.1.call-done = f32[96,4096]{1,0:T(8,128)} async-done(((f32[384,4096]{1,0:T(8,128)}), f32[96,4096]{1,0:T(8,128)}) %reduce-scatter.9.cloned.1.call-update) | async-done | bytes 1572880 | tf_op jit(solution)/shard_map/reduce_scatter | solution.py:221
  137.7 2.1 fusion.71
  142.0 2.7 collective-permute-start.2
  144.7 70.5 %reduce-scatter.11.cloned.1.call-done = f32[96,4096]{1,0:T(8,128)} async-done(((f32[384,4096]{1,0:T(8,128)}), f32[96,4096]{1,0:T(8,128)}) %reduce-scatter.11.cloned.1.call-update) | async-done | bytes 1572880 | tf_op jit(solution)/shard_map/reduce_scatter | solution.py:221
  216.9 2.1 fusion.75
  223.3 3.1 collective-permute-start.4
  229.0 4.9 collective-permute-done.3
  233.9 4.1 collective-permute-done.4
  238.0 18.5 %fusion.18 = f32[384,3584]{1,0:T(8,128)} fusion(bf16[384,4096]{1,0:T(8,128)(2,1)S(1)} %constant_dynamic-update-slice_fusion.10, bf16[2,4096,3584]{2,1,0:T(8,128)(2,1)} %param.18), kind=kOutput, calls=%fused_computation.18 | convolution fusion | flops 11274289152 | bytes 38010880 | tf_op jit(solution)/shard_map/dot_general | solution.py:228
  256.5 19.2 %multiply_convert_fusion.11 = bf16[384,3584]{1,0:T(8,128)(2,1)} fusion(f32[384,3584]{1,0:T(8,128)} %fusion.18, bf16[384,4096]{1,0:T(8,128)(2,1)S(1)} %constant_dynamic-update-slice_fusion.10, bf16[2,4096,3584]{2,1,0:T(8,128)(2,1)} %param.17), kind=kOutput, calls=%fused_computation.53.clone.clone.2 | convolution fusion | flops 11282546688 | bytes 40763392 | tf_op jit(solution)/shard_map/dot_general | solution.py:227
  275.8 19.4 %fusion.14 = f32[384,4096]{1,0:T(8,128)} fusion(bf16[2,3584,4096]{2,1,0:T(8,128)(2,1)} %param.19, bf16[384,3584]{1,0:T(8,128)(2,1)} %multiply_convert_fusion.11), kind=kOutput, calls=%fused_computation.14 | convolution fusion | flops 11274289152 | bytes 38404096 | tf_op jit(solution)/shard_map/dot_general | solution.py:230
  297.1 18.5 %fusion.20 = f32[384,3584]{1,0:T(8,128)} fusion(bf16[384,4096]{1,0:T(8,128)(2,1)S(1)} %copy-done.34, bf16[2,4096,3584]{2,1,0:T(8,128)(2,1)} %param.17), kind=kOutput, calls=%fused_computation.20 | convolution fusion | flops 11274289152 | bytes 38010880 | tf_op jit(solution)/shard_map/dot_general | solution.py:227
  315.6 19.1 %fusion.52.clone.5 = bf16[384,3584]{1,0:T(8,128)(2,1)} fusion(bf16[384,4096]{1,0:T(8,128)(2,1)S(1)} %copy-done.34, bf16[2,4096,3584]{2,1,0:T(8,128)(2,1)} %param.18, f32[384,3584]{1,0:T(8,128)} %fusion.20), kind=kOutput, calls=%fused_computation.51.clone.clone.clone.2 | convolution fusion | flops 11282546688 | bytes 40763392 | tf_op jit(solution)/shard_map/dot_general | solution.py:228
  334.7 19.6 %fusion.12 = f32[384,4096]{1,0:T(8,128)} fusion(bf16[2,3584,4096]{2,1,0:T(8,128)(2,1)} %param.19, bf16[384,3584]{1,0:T(8,128)(2,1)} %fusion.52.clone.5), kind=kOutput, calls=%fused_computation.12 | convolution fusion | flops 11274289152 | bytes 38404096 | tf_op jit(solution)/shard_map/dot_general | solution.py:230
  354.5 7.3 reduce-scatter.13.cloned.1.call-done
  367.4 58.2 %reduce-scatter.15.cloned.1.call-done = f32[96,4096]{1,0:T(8,128)} async-done(((f32[384,4096]{1,0:T(8,128)}), f32[96,4096]{1,0:T(8,128)}) %reduce-scatter.15.cloned.1.call-update) | async-done | bytes 1572880 | tf_op jit(solution)/shard_map/reduce_scatter | solution.py:221
  431.7 2.7 collective-permute-start.6
  434.3 2.2 copy-done.1
  436.5 2.5 copy-done.3
  439.0 10.0 pack_weights.3.w_ref
  449.3 10.5 collective-permute-done.5
  460.8 3.5 collective-permute-start.8
  464.5 15.0 %collective-permute-done.7 = bf16[48,4096]{1,0:T(8,128)(2,1)S(1)} collective-permute-done((bf16[48,4096]{1,0:T(8,128)(2,1)S(1)}, bf16[48,4096]{1,0:T(8,128)(2,1)S(1)}, u32[]{:S(2)}, u32[]{:S(2)}) %collective-permute-start.7) | collective-permute-done | bytes 393248 | tf_op jit(solution)/shard_map/ppermute | solution.py:210
  480.1 9.5 project.4
  491.8 9.6 all-to-all-start
  503.2 9.5 project.5
  514.7 15.7 %all-to-all-done.q_ref = bf16[8,3,384,128]{3,2,1,0:T(8,128)(2,1)S(1)} async-done(((bf16[8,3,384,128]{3,2,1,0:T(8,128)(2,1)}), bf16[8,3,384,128]{3,2,1,0:T(8,128)(2,1)S(1)}, u32[]{:S(2)}, u32[]{:S(2)}) %all-to-all-start) | async-done | bytes 2359328 | tf_op jit(solution)/shard_map/all_to_all | solution.py:305
  530.3 5.3 all-to-all-start.1
  536.6 28.2 %all-to-all-done.1.q_ref = bf16[8,3,384,128]{3,2,1,0:T(8,128)(2,1)} async-done(((bf16[8,3,384,128]{3,2,1,0:T(8,128)(2,1)}), bf16[8,3,384,128]{3,2,1,0:T(8,128)(2,1)}, u32[]{:S(2)}, u32[]{:S(2)}) %all-to-all-start.1) | async-done | bytes 2359328 | tf_op jit(solution)/shard_map/all_to_all | solution.py:305
  566.6 28.0 %global_attention.2 = bf16[8,384,128]{2,1,0:T(8,128)(2,1)S(1)} custom-call(bf16[8,3,384,128]{3,2,1,0:T(8,128)(2,1)S(1)} %all-to-all-done.q_ref, bf16[6144,128]{1,0:T(8,128)(2,1)S(1)} %bitcast.179, bf16[6144,128]{1,0:T(8,128)(2,1)S(1)} %bitcast.182), custom_call_target="tpu_custom_call" | custom-call | flops 9663676416 | bytes 6291456 | tf_op jit(solution)/shard_map/global_attention/pallas_call | solution.py:176
  594.6 15.6 %all_to_all.20 = bf16[8,384,128]{2,1,0:T(8,128)(2,1)S(1)} all-to-all(bf16[8,384,128]{2,1,0:T(8,128)(2,1)S(1)} %global_attention.2), channel_id=1, replica_groups=mesh['rep'=1,'tp'=4,'sp'=8] {'sp'}, dimensions={0} | all-to-all | bytes 1572864 | tf_op jit(solution)/shard_map/all_to_all | solution.py:310
  610.6 9.5 fusion.42
  622.0 30.4 %global_attention.3 = bf16[8,384,128]{2,1,0:T(8,128)(2,1)S(1)} custom-call(bf16[8,3,384,128]{3,2,1,0:T(8,128)(2,1)} %all-to-all-done.1.q_ref, bf16[6144,128]{1,0:T(8,128)(2,1)S(1)} %bitcast.181, bf16[6144,128]{1,0:T(8,128)(2,1)S(1)} %bitcast.184), custom_call_target="tpu_custom_call" | custom-call | flops 9663676416 | bytes 6291456 | tf_op jit(solution)/shard_map/global_attention/pallas_call | solution.py:176
  652.4 15.7 %all_to_all.21 = bf16[8,384,128]{2,1,0:T(8,128)(2,1)S(1)} all-to-all(bf16[8,384,128]{2,1,0:T(8,128)(2,1)S(1)} %global_attention.3), channel_id=1, replica_groups=mesh['rep'=1,'tp'=4,'sp'=8] {'sp'}, dimensions={0} | all-to-all | bytes 1572864 | tf_op jit(solution)/shard_map/all_to_all | solution.py:310
  668.4 9.7 fusion.41
  678.3 3.9 reduce-scatter.17.cloned.1.call-done
  689.2 2.8 collective-permute-start.10
  692.1 70.4 %reduce-scatter.19.cloned.1.call-done = f32[96,4096]{1,0:T(8,128)} async-done(((f32[384,4096]{1,0:T(8,128)}), f32[96,4096]{1,0:T(8,128)}) %reduce-scatter.19.cloned.1.call-update) | async-done | bytes 1572880 | tf_op jit(solution)/shard_map/reduce_scatter | solution.py:221
  768.4 2.7 collective-permute-start.12
  773.0 6.8 collective-permute-done.11
  781.9 19.4 %fusion.6 = f32[384,3584]{1,0:T(8,128)} fusion(bf16[384,4096]{1,0:T(8,128)(2,1)} %constant_dynamic-update-slice_fusion, bf16[2,4096,3584]{2,1,0:T(8,128)(2,1)} %param.18), kind=kOutput, calls=%fused_computation.6 | convolution fusion | flops 11274289152 | bytes 38010880 | tf_op jit(solution)/shard_map/dot_general | solution.py:228
  801.3 20.4 %multiply_convert_fusion.10 = bf16[384,3584]{1,0:T(8,128)(2,1)} fusion(f32[384,3584]{1,0:T(8,128)} %fusion.6, bf16[384,4096]{1,0:T(8,128)(2,1)} %constant_dynamic-update-slice_fusion, bf16[2,4096,3584]{2,1,0:T(8,128)(2,1)} %param.17), kind=kOutput, calls=%fused_computation.52.clone.clone.2 | convolution fusion | flops 11282546688 | bytes 40763392 | tf_op jit(solution)/shard_map/dot_general | solution.py:227
  821.7 19.5 %fusion.2 = f32[384,4096]{1,0:T(8,128)} fusion(bf16[2,3584,4096]{2,1,0:T(8,128)(2,1)} %param.19, bf16[384,3584]{1,0:T(8,128)(2,1)} %multiply_convert_fusion.10), kind=kOutput, calls=%fused_computation.2 | convolution fusion | flops 11274289152 | bytes 38404096 | tf_op jit(solution)/shard_map/dot_general | solution.py:230
  841.4 19.4 %fusion.8 = f32[384,3584]{1,0:T(8,128)} fusion(bf16[384,4096]{1,0:T(8,128)(2,1)} %all-gather.10.cloned.1.call-done, bf16[2,4096,3584]{2,1,0:T(8,128)(2,1)} %param.17), kind=kOutput, calls=%fused_computation.8 | convolution fusion | flops 11274289152 | bytes 38010880 | tf_op jit(solution)/shard_map/dot_general | solution.py:227
  860.8 47.1 %reduce-scatter.21.cloned.1.call-done = f32[96,4096]{1,0:T(8,128)} async-done(((f32[384,4096]{1,0:T(8,128)}), f32[96,4096]{1,0:T(8,128)}) %reduce-scatter.21.cloned.1.call-update) | async-done | bytes 1572880 | tf_op jit(solution)/shard_map/reduce_scatter | solution.py:221
  909.5 2.6 fusion.90
  912.2 20.3 %fusion.49.clone.5 = bf16[384,3584]{1,0:T(8,128)(2,1)} fusion(bf16[384,4096]{1,0:T(8,128)(2,1)} %all-gather.10.cloned.1.call-done, bf16[2,4096,3584]{2,1,0:T(8,128)(2,1)} %param.18, f32[384,3584]{1,0:T(8,128)} %fusion.8), kind=kOutput, calls=%fused_computation.50.clone.clone.clone.2 | convolution fusion | flops 11282546688 | bytes 40763392 | tf_op jit(solution)/shard_map/dot_general | solution.py:228
  932.6 19.5 %fusion = f32[384,4096]{1,0:T(8,128)} fusion(bf16[2,3584,4096]{2,1,0:T(8,128)(2,1)} %param.19, bf16[384,3584]{1,0:T(8,128)(2,1)} %fusion.49.clone.5), kind=kOutput, calls=%fused_computation | convolution fusion | flops 11274289152 | bytes 38404096 | tf_op jit(solution)/shard_map/dot_general | solution.py:230
  952.2 61.2 %reduce-scatter.23.cloned.1.call-done = f32[96,4096]{1,0:T(8,128)} async-done(((f32[384,4096]{1,0:T(8,128)}), f32[96,4096]{1,0:T(8,128)}) %reduce-scatter.23.cloned.1.call-update) | async-done | bytes 1572880 | tf_op jit(solution)/shard_map/reduce_scatter | solution.py:221
  1015.0 2.6 fusion.94
  1022.5 12.8 %collective-permute-done.14 = bf16[2,512,128]{2,1,0:T(8,128)(2,1)} collective-permute-done((bf16[2,512,128]{2,1,0:T(8,128)(2,1)S(1)}, bf16[2,512,128]{2,1,0:T(8,128)(2,1)}, u32[]{:S(2)}, u32[]{:S(2)}) %collective-permute-start.14) | collective-permute-done | bytes 262176 | tf_op jit(solution)/shard_map/ppermute | solution.py:291
  1041.2 13.1 %all-gather.14.cloned.1.call-done = bf16[384,4096]{1,0:T(8,128)(2,1)} async-done(((bf16[96,4096]{1,0:T(8,128)(2,1)}), bf16[384,4096]{1,0:T(8,128)(2,1)}) %all-gather.14.cloned.1.call-update) | async-done | bytes 3145744 | tf_op jit(solution)/shard_map/all_gather | solution.py:195
  1054.4 5.3 pad_maximum_fusion
  (203 shorter events, 76.8 us)
Async XLA Ops:
  7.2 128.9 %reduce-scatter.9.cloned.1.call-start = ((), (), s32[]{:S(2)}) async-start(), calls=%async_computation.12 | async-start | bytes 7864320 | tf_op jit(solution)/shard_map/reduce_scatter | solution.py:221
  9.3 4.2 copy-start.33
  9.3 4.6 copy-start.12
  13.9 7.2 copy-start.2
  16.7 4.4 copy-start
  44.6 6.3 copy-start.24
  44.7 10.7 %collective-permute-start = (bf16[4,512,128]{2,1,0:T(8,128)(2,1)S(1)}, bf16[4,512,128]{2,1,0:T(8,128)(2,1)S(1)}, u32[]{:S(2)}, u32[]{:S(2)}) collective-permute-start(bf16[4,512,128]{2,1,0:T(8,128)(2,1)S(1)} %slice.184), channel_id=1, source_target_pairs={{0,1},{1,2},{2,3},{3,4},{4,5},{5,6},{6,7},{8,9},{9,10},{10,11},{11... | collective-permute-start | bytes 1572872 | tf_op jit(solution)/shard_map/ppermute | solution.py:275
  49.5 1.4 copy-start.4
  50.9 4.5 copy-start.5
  70.8 144.4 %reduce-scatter.11.cloned.1.call-start = ((), (), s32[]{:S(2)}) async-start(), calls=%async_computation.13 | async-start | bytes 7864320 | tf_op jit(solution)/shard_map/reduce_scatter | solution.py:221
  70.9 1.7 copy-start.6
  89.0 206.2 %all-gather.6.cloned.1.call-start = ((), (), s32[]{:S(2)}) async-start(), calls=%async_computation.14 | async-start | bytes 3932160 | tf_op jit(solution)/shard_map/all_gather | solution.py:195
  139.9 1.0 copy-start.17
  142.0 79.1 %collective-permute-start.1 = (bf16[96,4096]{1,0:T(8,128)(2,1)}, bf16[96,4096]{1,0:T(8,128)(2,1)}, u32[]{:S(2)}, u32[]{:S(2)}) collective-permute-start(bf16[96,4096]{1,0:T(8,128)(2,1)} %get-tuple-element.38), channel_id=1, source_target_pairs={{0,8},{8,16},{16,24},{24,0},{1,9},{9,17},{17,25},{25,1},{2,10},{10... | collective-permute-start | bytes 2359304 | tf_op jit(solution)/shard_map/ppermute | solution.py:208
  142.0 80.3 %collective-permute-start.2 = (bf16[96,4096]{1,0:T(8,128)(2,1)}, bf16[96,4096]{1,0:T(8,128)(2,1)}, u32[]{:S(2)}, u32[]{:S(2)}) collective-permute-start(bf16[96,4096]{1,0:T(8,128)(2,1)} %get-tuple-element.38), channel_id=1, source_target_pairs={{0,24},{8,0},{16,8},{24,16},{1,25},{9,1},{17,9},{25,17},{2,26},{10... | collective-permute-start | bytes 2359304 | tf_op jit(solution)/shard_map/ppermute | solution.py:209
  221.1 140.7 %reduce-scatter.13.cloned.1.call-start = ((), (), s32[]{:S(2)}) async-start(), calls=%async_computation.15 | async-start | bytes 7864320 | tf_op jit(solution)/shard_map/reduce_scatter | solution.py:221
  222.2 11.7 %collective-permute-start.3 = (bf16[48,4096]{1,0:T(8,128)(2,1)S(1)}, bf16[48,4096]{1,0:T(8,128)(2,1)S(1)}, u32[]{:S(2)}, u32[]{:S(2)}) collective-permute-start(bf16[48,4096]{1,0:T(8,128)(2,1)S(1)} %slice.187), channel_id=1, source_target_pairs={{0,8},{8,16},{16,24},{24,0},{1,9},{9,17},{17,25},{25,1},{2,10},{10... | collective-permute-start | bytes 1179656 | tf_op jit(solution)/shard_map/ppermute | solution.py:210
  223.3 14.6 %collective-permute-start.4 = (bf16[48,4096]{1,0:T(8,128)(2,1)S(1)}, bf16[48,4096]{1,0:T(8,128)(2,1)S(1)}, u32[]{:S(2)}, u32[]{:S(2)}) collective-permute-start(bf16[48,4096]{1,0:T(8,128)(2,1)S(1)} %slice.188), channel_id=1, source_target_pairs={{0,24},{8,0},{16,8},{24,16},{1,25},{9,1},{17,9},{25,17},{2,26},{10... | collective-permute-start | bytes 1179656 | tf_op jit(solution)/shard_map/ppermute | solution.py:211
  295.2 1.9 copy-start.34
  295.2 130.5 %reduce-scatter.15.cloned.1.call-start = ((), (), s32[]{:S(2)}) async-start(), calls=%async_computation.16 | async-start | bytes 7864320 | tf_op jit(solution)/shard_map/reduce_scatter | solution.py:221
  354.3 9.0 copy-start.18
  354.4 9.0 copy-start.32
  354.4 146.9 %all-gather.8.cloned.1.call-start = ((), (), s32[]{:S(2)}) async-start(), calls=%async_computation.17 | async-start | bytes 3932160 | tf_op jit(solution)/shard_map/all_gather | solution.py:195
  363.4 2.8 copy-start.31
  429.4 0.9 copy-start.13
  431.5 17.5 %copy-start.25 = (f32[768,64]{1,0:T(8,128)S(1)}, f32[768,64]{1,0:T(8,128)}, u32[]{:S(2)}) copy-start(f32[768,64]{1,0:T(8,128)} %get-tuple-element.63) | copy-start | bytes 589828
  431.6 28.3 %collective-permute-start.5 = (bf16[96,4096]{1,0:T(8,128)(2,1)}, bf16[96,4096]{1,0:T(8,128)(2,1)S(1)}, u32[]{:S(2)}, u32[]{:S(2)}) collective-permute-start(bf16[96,4096]{1,0:T(8,128)(2,1)} %get-tuple-element.32), channel_id=1, source_target_pairs={{0,8},{8,16},{16,24},{24,0},{1,9},{9,17},{17,25},{25,1},{2,10},{10... | collective-permute-start | bytes 2359304 | tf_op jit(solution)/shard_map/ppermute | solution.py:208
  431.7 29.1 %collective-permute-start.6 = (bf16[96,4096]{1,0:T(8,128)(2,1)}, bf16[96,4096]{1,0:T(8,128)(2,1)S(1)}, u32[]{:S(2)}, u32[]{:S(2)}) collective-permute-start(bf16[96,4096]{1,0:T(8,128)(2,1)} %get-tuple-element.32), channel_id=1, source_target_pairs={{0,24},{8,0},{16,8},{24,16},{1,25},{9,1},{17,9},{25,17},{2,26},{10... | collective-permute-start | bytes 2359304 | tf_op jit(solution)/shard_map/ppermute | solution.py:209
  434.3 2.2 copy-start.1
  436.5 2.5 copy-start.3
  439.0 10.0 copy-start.26
  439.0 10.0 copy-start.27
  459.9 19.7 %collective-permute-start.7 = (bf16[48,4096]{1,0:T(8,128)(2,1)S(1)}, bf16[48,4096]{1,0:T(8,128)(2,1)S(1)}, u32[]{:S(2)}, u32[]{:S(2)}) collective-permute-start(bf16[48,4096]{1,0:T(8,128)(2,1)S(1)} %slice.189), channel_id=1, source_target_pairs={{0,8},{8,16},{16,24},{24,0},{1,9},{9,17},{17,25},{25,1},{2,10},{10... | collective-permute-start | bytes 1179656 | tf_op jit(solution)/shard_map/ppermute | solution.py:210
  460.8 19.2 %collective-permute-start.8 = (bf16[48,4096]{1,0:T(8,128)(2,1)S(1)}, bf16[48,4096]{1,0:T(8,128)(2,1)S(1)}, u32[]{:S(2)}, u32[]{:S(2)}) collective-permute-start(bf16[48,4096]{1,0:T(8,128)(2,1)S(1)} %slice.190), channel_id=1, source_target_pairs={{0,24},{8,0},{16,8},{24,16},{1,25},{9,1},{17,9},{25,17},{2,26},{10... | collective-permute-start | bytes 1179656 | tf_op jit(solution)/shard_map/ppermute | solution.py:211
  491.8 38.6 %all-to-all-start = ((bf16[8,3,384,128]{3,2,1,0:T(8,128)(2,1)}), bf16[8,3,384,128]{3,2,1,0:T(8,128)(2,1)S(1)}, u32[]{:S(2)}, u32[]{:S(2)}) async-start(bf16[8,3,384,128]{3,2,1,0:T(8,128)(2,1)} %copy.25), calls=%async_computation.3 | async-start | bytes 4718592 | tf_op jit(solution)/shard_map/all_to_all | solution.py:305
  501.3 1.9 copy-start.11
  530.3 34.5 %all-to-all-start.1 = ((bf16[8,3,384,128]{3,2,1,0:T(8,128)(2,1)}), bf16[8,3,384,128]{3,2,1,0:T(8,128)(2,1)}, u32[]{:S(2)}, u32[]{:S(2)}) async-start(bf16[8,3,384,128]{3,2,1,0:T(8,128)(2,1)} %pad_maximum_fusion.2), calls=%async_computation.5 | async-start | bytes 4718592 | tf_op jit(solution)/shard_map/all_to_all | solution.py:305
  535.6 146.6 %reduce-scatter.17.cloned.1.call-start = ((), (), s32[]{:S(2)}) async-start(), calls=%async_computation.18 | async-start | bytes 7864320 | tf_op jit(solution)/shard_map/reduce_scatter | solution.py:221
  564.8 1.6 copy-start.23
  566.5 28.1 %copy-start.7 = (bf16[8,768,128]{2,1,0:T(8,128)(2,1)}, bf16[8,768,128]{2,1,0:T(8,128)(2,1)S(1)}, u32[]{:S(2)}) copy-start(bf16[8,768,128]{2,1,0:T(8,128)(2,1)S(1)} %pad_maximum_fusion.3) | copy-start | bytes 4718596
  566.6 28.0 %copy-start.9 = (bf16[8,768,128]{2,1,0:T(8,128)(2,1)}, bf16[8,768,128]{2,1,0:T(8,128)(2,1)S(1)}, u32[]{:S(2)}) copy-start(bf16[8,768,128]{2,1,0:T(8,128)(2,1)S(1)} %pad_maximum_fusion.4) | copy-start | bytes 4718596
  620.1 1.4 copy-start.8
  620.1 1.9 copy-start.10
  620.2 142.3 %reduce-scatter.19.cloned.1.call-start = ((), (), s32[]{:S(2)}) async-start(), calls=%async_computation.19 | async-start | bytes 7864320 | tf_op jit(solution)/shard_map/reduce_scatter | solution.py:221
  678.1 5.7 copy-start.16
  678.1 5.7 copy-start.30
  678.2 163.0 %all-gather.10.cloned.1.call-start = ((), (), s32[]{:S(2)}) async-start(), calls=%async_computation.20 | async-start | bytes 3932160 | tf_op jit(solution)/shard_map/all_gather | solution.py:195
  683.8 4.0 copy-start.29
  685.8 78.3 %copy-start.14 = (bf16[96,4096]{1,0:T(8,128)(2,1)S(1)}, bf16[96,4096]{1,0:T(8,128)(2,1)}, u32[]{:S(2)}) copy-start(bf16[96,4096]{1,0:T(8,128)(2,1)} %copy-done.13) | copy-start | bytes 2359300
  689.2 78.9 %collective-permute-start.9 = (bf16[96,4096]{1,0:T(8,128)(2,1)}, bf16[96,4096]{1,0:T(8,128)(2,1)S(1)}, u32[]{:S(2)}, u32[]{:S(2)}) collective-permute-start(bf16[96,4096]{1,0:T(8,128)(2,1)} %get-tuple-element.26), channel_id=1, source_target_pairs={{0,8},{8,16},{16,24},{24,0},{1,9},{9,17},{17,25},{25,1},{2,10},{10... | collective-permute-start | bytes 2359304 | tf_op jit(solution)/shard_map/ppermute | solution.py:208
  689.2 79.1 %collective-permute-start.10 = (bf16[96,4096]{1,0:T(8,128)(2,1)}, bf16[96,4096]{1,0:T(8,128)(2,1)S(1)}, u32[]{:S(2)}, u32[]{:S(2)}) collective-permute-start(bf16[96,4096]{1,0:T(8,128)(2,1)} %get-tuple-element.26), channel_id=1, source_target_pairs={{0,24},{8,0},{16,8},{24,16},{1,25},{9,1},{17,9},{25,17},{2,26},{10... | collective-permute-start | bytes 2359304 | tf_op jit(solution)/shard_map/ppermute | solution.py:209
  766.0 0.9 copy-start.19
  768.1 139.8 %reduce-scatter.21.cloned.1.call-start = ((), (), s32[]{:S(2)}) async-start(), calls=%async_computation.21 | async-start | bytes 7864320 | tf_op jit(solution)/shard_map/reduce_scatter | solution.py:221
  768.2 11.6 %collective-permute-start.11 = (bf16[48,4096]{1,0:T(8,128)(2,1)S(1)}, bf16[48,4096]{1,0:T(8,128)(2,1)S(1)}, u32[]{:S(2)}, u32[]{:S(2)}) collective-permute-start(bf16[48,4096]{1,0:T(8,128)(2,1)S(1)} %slice.204), channel_id=1, source_target_pairs={{0,8},{8,16},{16,24},{24,0},{1,9},{9,17},{17,25},{25,1},{2,10},{10... | collective-permute-start | bytes 1179656 | tf_op jit(solution)/shard_map/ppermute | solution.py:210
  768.4 12.7 %collective-permute-start.12 = (bf16[48,4096]{1,0:T(8,128)(2,1)S(1)}, bf16[48,4096]{1,0:T(8,128)(2,1)S(1)}, u32[]{:S(2)}, u32[]{:S(2)}) collective-permute-start(bf16[48,4096]{1,0:T(8,128)(2,1)S(1)} %slice.205), channel_id=1, source_target_pairs={{0,24},{8,0},{16,8},{24,16},{1,25},{9,1},{17,9},{25,17},{2,26},{10... | collective-permute-start | bytes 1179656 | tf_op jit(solution)/shard_map/ppermute | solution.py:211
  841.3 68.2 %copy-start.28 = (f32[1,1,4096]{2,1,0:T(1,128)S(1)}, f32[1,1,4096]{2,1,0:T(1,128)}, u32[]{:S(2)}) copy-start(f32[1,1,4096]{2,1,0:T(1,128)} %get-tuple-element.55) | copy-start | bytes 49156
  841.3 110.8 %all-gather.12.cloned.1.call-start = ((), (), s32[]{:S(2)}) async-start(), calls=%async_computation.22 | async-start | bytes 3932160 | tf_op jit(solution)/shard_map/all_gather | solution.py:195
  912.2 101.2 %reduce-scatter.23.cloned.1.call-start = ((), (), s32[]{:S(2)}) async-start(), calls=%async_computation.23 | async-start | bytes 7864320 | tf_op jit(solution)/shard_map/reduce_scatter | solution.py:221
  952.0 62.9 %copy-start.20 = (bf16[96,4096]{1,0:T(8,128)(2,1)S(1)}, bf16[96,4096]{1,0:T(8,128)(2,1)}, u32[]{:S(2)}) copy-start(bf16[96,4096]{1,0:T(8,128)(2,1)} %copy-done.19) | copy-start | bytes 2359300
  952.1 102.3 %all-gather.14.cloned.1.call-start = ((), (), s32[]{:S(2)}) async-start(), calls=%async_computation.24 | async-start | bytes 3932160 | tf_op jit(solution)/shard_map/all_gather | solution.py:195
  1017.6 36.8 %copy-start.22 = (bf16[384,4096]{1,0:T(8,128)(2,1)S(1)}, bf16[384,4096]{1,0:T(8,128)(2,1)}, u32[]{:S(2)}) copy-start(bf16[384,4096]{1,0:T(8,128)(2,1)} %all-gather.12.cloned.1.call-done) | copy-start | bytes 9437188
  1018.8 1.4 collective-permute-start.13
  1021.1 14.1 %collective-permute-start.14 = (bf16[2,512,128]{2,1,0:T(8,128)(2,1)S(1)}, bf16[2,512,128]{2,1,0:T(8,128)(2,1)}, u32[]{:S(2)}, u32[]{:S(2)}) collective-permute-start(bf16[2,512,128]{2,1,0:T(8,128)(2,1)S(1)} %fusion.96), channel_id=1, source_target_pairs={{3,1},{7,5},{11,9},{15,13},{19,17},{23,21},{27,25},{31,29}} | collective-permute-start | bytes 786440 | tf_op jit(solution)/shard_map/ppermute | solution.py:291
  1036.9 2.7 collective-permute-start.15
  (2 other events, 1.8 us)
Sparse Core Ops, SparseCore 0:
  70.9 65.1 reduce-scatter.8
  139.0 76.1 reduce-scatter.10
  221.2 39.5 all-gather.5
  295.3 66.3 reduce-scatter.12
  364.5 61.1 reduce-scatter.14
  431.7 54.8 all-gather.7
  620.3 61.8 reduce-scatter.16
  685.1 77.3 reduce-scatter.18
  768.2 37.8 all-gather.9
  841.4 66.4 reduce-scatter.20
  912.3 36.5 all-gather.11
  952.2 61.0 reduce-scatter.22
  1017.8 36.5 all-gather.13
